TPU v7x, 128 devices: a whole 4x4x4 slice. The times are simulated.
128 devices in a mesh: batch: 1, cols: 64 (over z, y, x), rows: 2 (over core).
Axes of the slice: x: 4, y: 4, z: 4, core: 2. Of those that a mesh axis runs over, the one named last changes fastest.
Arguments:
- frames: bfloat16 [4, 16, 16, 512, 384], P(None, 'batch', 'rows', 'cols')
- h_init: float32 [16, 16, 512, 384], P('batch', 'rows', 'cols')
- w_x: bfloat16 [3, 3, 384, 1152], replicated
- w_hzr: bfloat16 [3, 3, 384, 768], replicated
- w_hn: bfloat16 [3, 3, 384, 384], replicated
- gate_bias: float32 [1152], replicated
Outputs:
- output 1: bfloat16 [4, 16, 16, 512, 384], P(None, 'batch', 'rows', 'cols')
- output 2: float32 [16, 16, 512, 384], P('batch', 'rows', 'cols')
All inputs are finite; a program needn't handle non-finite values.
Results may differ from a plain program's by a relative error of at most 0.00190342.
Values are sent between devices in bfloat16 or wider.
A program may use at most 1 GiB of HBM per device.

v0:
```python
import jax
import jax.numpy as jnp
from jax import lax
from jax.sharding import PartitionSpec as P, NamedSharding


def with_halo(tile, width, n_rows, n_cols):
    tile_h = tile.shape[-3]
    tile_w = tile.shape[-2]
    down_pairs = [(dev_idx, dev_idx + 1) for dev_idx in range(n_rows - 1)]
    up_pairs = [(dev_idx + 1, dev_idx) for dev_idx in range(n_rows - 1)]
    from_above = lax.ppermute(tile[..., tile_h - width:, :, :], 'rows', down_pairs)
    from_below = lax.ppermute(tile[..., :width, :, :], 'rows', up_pairs)
    tall_tile = jnp.concatenate([from_above, tile, from_below], axis=-3)
    right_pairs = [(dev_idx, dev_idx + 1) for dev_idx in range(n_cols - 1)]
    left_pairs = [(dev_idx + 1, dev_idx) for dev_idx in range(n_cols - 1)]
    from_left = lax.ppermute(tall_tile[..., tile_w - width:, :], 'cols', right_pairs)
    from_right = lax.ppermute(tall_tile[..., :width, :], 'cols', left_pairs)
    return jnp.concatenate([from_left, tall_tile, from_right], axis=-2)


def im2col_conv(padded, w_mat):
    out_h = padded.shape[-3] - 2
    out_w = padded.shape[-2] - 2
    tap_list = [padded[..., row_off:row_off + out_h, col_off:col_off + out_w, :] for row_off in range(3) for col_off in range(3)]
    patches = jnp.concatenate(tap_list, axis=-1)
    return jnp.einsum('...k,kg->...g', patches, w_mat, preferred_element_type=jnp.float32)


def solution(mesh):
    n_rows = mesh.shape['rows']
    n_cols = mesh.shape['cols']
    frame_spec = P(None, 'batch', 'rows', 'cols', None)
    state_spec = P('batch', 'rows', 'cols', None)

    def local_fn(frames, h_init, w_x, w_hzr, w_hn, gate_bias):
        n_hidden = h_init.shape[-1]
        wx_mat = w_x.reshape(-1, w_x.shape[-1])
        whzr_mat = w_hzr.reshape(-1, w_hzr.shape[-1])
        whn_mat = w_hn.reshape(-1, w_hn.shape[-1])
        frames_pad = with_halo(frames, 1, n_rows, n_cols)

        def one_step(h_prev, frame_pad):
            gate_x = im2col_conv(frame_pad, wx_mat) + gate_bias
            h_pad = with_halo(h_prev.astype(jnp.bfloat16), 1, n_rows, n_cols)
            zr_gates = jax.nn.sigmoid(gate_x[..., :2 * n_hidden] + im2col_conv(h_pad, whzr_mat))
            update = zr_gates[..., :n_hidden]
            reset_pad = with_halo((zr_gates[..., n_hidden:] * h_prev).astype(jnp.bfloat16), 1, n_rows, n_cols)
            candidate = jnp.tanh(gate_x[..., 2 * n_hidden:] + im2col_conv(reset_pad, whn_mat))
            h_next = (1.0 - update) * candidate + update * h_prev
            return h_next, h_next.astype(jnp.bfloat16)

        h_last, h_seq = lax.scan(one_step, h_init, frames_pad)
        return h_seq, h_last

    return jax.shard_map(local_fn, mesh=mesh, in_specs=(frame_spec, state_spec, P(), P(), P(), P()), out_specs=(frame_spec, state_spec), check_vma=False)
```

profile of v0, /device:TPU:97, one launch (start us, length us, event | category | flops | bytes accessed | tf_op | source)
XLA Modules:
  0.0 339.0 jit_solution(4236502946545770792)
XLA Ops:
  3.4 3.1 collective-permute-start.9
  6.6 3.2 constant_dynamic-update-slice_fusion.3
  9.9 1.9 copy-done.4
  12.7 3.1 collective-permute-start.10
  15.8 6.4 %collective-permute-start.11 = (bf16[4,16,10,1,384]{4,1,3,2,0:T(8,128)(2,1)S(1)}, bf16[4,16,10,1,384]{4,1,3,2,0:T(8,128)(2,1)S(1)}, u32[]{:S(2)}, u32[]{:S(2)}) collective-permute-start(bf16[4,16,10,1,384]{4,1,3,2,0:T(8,128)(2,1)S(1)} %get-tuple-element.86), channel_id=1, source_target_pairs={{2,0},{4,2},{6,4},{8,6},{10,8},{12,10},{14,12},{16,14},{18,16},{20... | collective-permute-start | bytes 1474568 | tf_op jit(solution)/shard_map/ppermute | solution.py:18
  22.3 9.5 %collective-permute-done.10 = bf16[4,16,10,1,384]{4,1,3,2,0:T(8,128)(2,1)S(1)} collective-permute-done((bf16[4,16,10,1,384]{4,1,3,2,0:T(8,128)(2,1)}, bf16[4,16,10,1,384]{4,1,3,2,0:T(8,128)(2,1)S(1)}, u32[]{:S(2)}, u32[]{:S(2)}) %collective-permute-start.10) | collective-permute-done | bytes 491552 | tf_op jit(solution)/shard_map/ppermute | solution.py:17
  33.1 5.0 %pad_maximum_fusion.12 = bf16[4,16,10,10,384]{4,1,3,2,0:T(8,128)(2,1)} fusion(bf16[4,16,10,1,384]{4,1,3,2,0:T(8,128)(2,1)S(1)} %collective-permute-done.11, bf16[4,16,10,8,384]{4,1,3,2,0:T(8,128)(2,1)} %copy-done.4, bf16[4,16,10,1,384]{4,1,3,2,0:T(8,128)(2,1)S(1)} %collective-permute-done.10), kind=kLoop, calls=%fused_computation.62 | loop fusion | flops 4915200 | bytes 9830400 | tf_op jit(solution)/shard_map/concatenate | solution.py:19
  38.1 299.7 %while.12 = (s32[]{:T(128)}, f32[16,8,8,384]{3,2,1,0:T(8,128)S(1)}, bf16[4,16,8,8,384]{4,3,2,1,0:T(8,128)(2,1)}, bf16[4,16,10,10,384]{4,1,3,2,0:T(8,128)(2,1)}, ...) while((s32[]{:T(128)}, f32[16,8,8,384]{3,2,1,0:T(8,128)S(1)}, ...), condition=%wide.region_1.2_spmd, body=%wide.region_0.1_spmd.sunk | while | flops 16341172224 | bytes 218240144 | solution.py:53
  38.3 2.5 collective-permute-start
  46.7 8.3 %collective-permute-start.2 = (bf16[16,10,1,384]{3,2,1,0:T(2,128)(2,1)S(1)}, bf16[16,10,1,384]{3,2,1,0:T(2,128)(2,1)S(1)}, u32[]{:S(2)}, u32[]{:S(2)}) collective-permute-start(bf16[16,10,1,384]{3,2,1,0:T(2,128)(2,1)S(1)} %get-tuple-element.154), channel_id=1, source_target_pairs={{2,0},{4,2},{6,4},{8,6},{10,8},{12,10},{14,12},{16,14},{18,16},{20... | collective-permute-start | bytes 368648 | tf_op jit(solution)/shard_map/while/body/eval_jaxpr/ppermute | solution.py:18
  55.1 1.9 collective-permute-start.3
  57.0 9.6 %fusion.51 = f32[16,8,8,1152]{3,2,1,0:T(8,128)S(1)} fusion(bf16[16,8,8,3456]{3,2,1,0:T(8,128)(2,1)S(1)} %slice_dynamic-update-slice_fusion.50, bf16[3456,1152]{1,0:T(8,128)(2,1)S(1)} %bitcast.61, f32[1152]{0:T(1024)S(1)} %get-tuple-element.189), kind=kOutput, calls=%fused_computation.4.clone.1 | convolution fusion | flops 8154906624 | bytes 19763712 | tf_op jit(solution)/shard_map/while/body/eval_jaxpr/...k,kg->...g/dot_general | solution.py:27
  67.3 1.5 pad_maximum_fusion.18
  71.6 6.1 %fusion.55 = f32[16,8,8,768]{3,2,1,0:T(8,128)S(1)} fusion(f32[16,8,8,1152]{3,2,1,0:T(8,128)S(1)} %fusion.51, bf16[16,8,8,3456]{3,2,1,0:T(8,128)(2,1)S(1)} %slice_dynamic-update-slice_fusion.56, bf16[3456,768]{1,0:T(8,128)(2,1)S(1)} %bitcast.64), kind=kOutput, calls=%fused_computation.9.clone.1 | convolution fusion | flops 5438963712 | bytes 18677760 | tf_op jit(solution)/shard_map/while/body/eval_jaxpr/...k,kg->...g/dot_general | solution.py:27
  78.1 4.9 %collective-permute-start.4 = (bf16[16,1,8,384]{3,2,1,0:T(8,128)(2,1)S(1)}, bf16[16,1,8,384]{3,2,1,0:T(8,128)(2,1)S(1)}, u32[]{:S(2)}, u32[]{:S(2)}) collective-permute-start(bf16[16,1,8,384]{3,2,1,0:T(8,128)(2,1)S(1)} %get-tuple-element.158), channel_id=1, source_target_pairs={{1,0},{3,2},{5,4},{7,6},{9,8},{11,10},{13,12},{15,14},{17,16},{19,... | collective-permute-start | bytes 294920 | tf_op jit(solution)/shard_map/while/body/eval_jaxpr/ppermute | solution.py:13
  84.3 1.9 collective-permute-done.5
  86.5 5.7 %collective-permute-start.6 = (bf16[16,10,1,384]{3,2,1,0:T(2,128)(2,1)S(1)}, bf16[16,10,1,384]{3,2,1,0:T(2,128)(2,1)S(1)}, u32[]{:S(2)}, u32[]{:S(2)}) collective-permute-start(bf16[16,10,1,384]{3,2,1,0:T(2,128)(2,1)S(1)} %get-tuple-element.160), channel_id=1, source_target_pairs={{2,0},{4,2},{6,4},{8,6},{10,8},{12,10},{14,12},{16,14},{18,16},{20... | collective-permute-start | bytes 368648 | tf_op jit(solution)/shard_map/while/body/eval_jaxpr/ppermute | solution.py:18
  92.1 1.9 collective-permute-start.7
  94.1 3.2 collective-permute-done.6
  97.3 8.1 %collective-permute-done.7 = bf16[16,10,1,384]{3,2,1,0:T(2,128)(2,1)S(1)} collective-permute-done((bf16[16,10,1,384]{3,2,1,0:T(2,128)(2,1)S(1)}, bf16[16,10,1,384]{3,2,1,0:T(2,128)(2,1)S(1)}, u32[]{:S(2)}, u32[]{:S(2)}) %collective-permute-start.7) | collective-permute-done | bytes 122912 | tf_op jit(solution)/shard_map/while/body/eval_jaxpr/ppermute | solution.py:17
  105.3 1.5 pad_maximum_fusion.20
  110.4 6.8 %bitcast_dynamic-update-slice_fusion.2 = (bf16[4,16,8,8,384]{4,3,2,1,0:T(8,128)(2,1)}, f32[16,8,8,384]{3,2,1,0:T(8,128)S(1)}) fusion(bf16[4,16,8,8,384]{4,3,2,1,0:T(8,128)(2,1)} %get-tuple-element.177, s32[]{:T(128)S(6)} %copy.53, f32[16,8,8,384]{3,2,1,0:T(8,128)S(1)} %get-tuple-element.176, ...), kind=kOutput, calls=%fused_computation.52.clone.1 | convolution fusion | flops 2720268288 | bytes 16809988 | tf_op jit(solution)/shard_map/while/body/eval_jaxpr/...k,kg->...g/dot_general | solution.py:27
  117.3 3.7 %collective-permute-start = (bf16[16,1,8,384]{3,2,1,0:T(8,128)(2,1)S(1)}, bf16[16,1,8,384]{3,2,1,0:T(8,128)(2,1)S(1)}, u32[]{:S(2)}, u32[]{:S(2)}) collective-permute-start(bf16[16,1,8,384]{3,2,1,0:T(8,128)(2,1)S(1)} %get-tuple-element.152), channel_id=1, source_target_pairs={{1,0},{3,2},{5,4},{7,6},{9,8},{11,10},{13,12},{15,14},{17,16},{19,... | collective-permute-start | bytes 294920 | tf_op jit(solution)/shard_map/while/body/eval_jaxpr/ppermute | solution.py:13
  127.0 1.9 collective-permute-start.2
  128.9 3.4 collective-permute-start.3
  132.3 9.5 %fusion.51 = f32[16,8,8,1152]{3,2,1,0:T(8,128)S(1)} fusion(bf16[16,8,8,3456]{3,2,1,0:T(8,128)(2,1)S(1)} %slice_dynamic-update-slice_fusion.50, bf16[3456,1152]{1,0:T(8,128)(2,1)S(1)} %bitcast.61, f32[1152]{0:T(1024)S(1)} %get-tuple-element.189), kind=kOutput, calls=%fused_computation.4.clone.1 | convolution fusion | flops 8154906624 | bytes 19763712 | tf_op jit(solution)/shard_map/while/body/eval_jaxpr/...k,kg->...g/dot_general | solution.py:27
  141.9 1.5 pad_maximum_fusion.18
  146.2 6.1 %fusion.55 = f32[16,8,8,768]{3,2,1,0:T(8,128)S(1)} fusion(f32[16,8,8,1152]{3,2,1,0:T(8,128)S(1)} %fusion.51, bf16[16,8,8,3456]{3,2,1,0:T(8,128)(2,1)S(1)} %slice_dynamic-update-slice_fusion.56, bf16[3456,768]{1,0:T(8,128)(2,1)S(1)} %bitcast.64), kind=kOutput, calls=%fused_computation.9.clone.1 | convolution fusion | flops 5438963712 | bytes 18677760 | tf_op jit(solution)/shard_map/while/body/eval_jaxpr/...k,kg->...g/dot_general | solution.py:27
  152.7 4.0 %collective-permute-start.4 = (bf16[16,1,8,384]{3,2,1,0:T(8,128)(2,1)S(1)}, bf16[16,1,8,384]{3,2,1,0:T(8,128)(2,1)S(1)}, u32[]{:S(2)}, u32[]{:S(2)}) collective-permute-start(bf16[16,1,8,384]{3,2,1,0:T(8,128)(2,1)S(1)} %get-tuple-element.158), channel_id=1, source_target_pairs={{1,0},{3,2},{5,4},{7,6},{9,8},{11,10},{13,12},{15,14},{17,16},{19,... | collective-permute-start | bytes 294920 | tf_op jit(solution)/shard_map/while/body/eval_jaxpr/ppermute | solution.py:13
  158.1 1.9 collective-permute-done.5
  160.3 5.4 %collective-permute-start.6 = (bf16[16,10,1,384]{3,2,1,0:T(2,128)(2,1)S(1)}, bf16[16,10,1,384]{3,2,1,0:T(2,128)(2,1)S(1)}, u32[]{:S(2)}, u32[]{:S(2)}) collective-permute-start(bf16[16,10,1,384]{3,2,1,0:T(2,128)(2,1)S(1)} %get-tuple-element.160), channel_id=1, source_target_pairs={{2,0},{4,2},{6,4},{8,6},{10,8},{12,10},{14,12},{16,14},{18,16},{20... | collective-permute-start | bytes 368648 | tf_op jit(solution)/shard_map/while/body/eval_jaxpr/ppermute | solution.py:18
  165.7 1.9 collective-permute-start.7
  167.6 3.2 collective-permute-done.6
  170.8 8.1 %collective-permute-done.7 = bf16[16,10,1,384]{3,2,1,0:T(2,128)(2,1)S(1)} collective-permute-done((bf16[16,10,1,384]{3,2,1,0:T(2,128)(2,1)S(1)}, bf16[16,10,1,384]{3,2,1,0:T(2,128)(2,1)S(1)}, u32[]{:S(2)}, u32[]{:S(2)}) %collective-permute-start.7) | collective-permute-done | bytes 122912 | tf_op jit(solution)/shard_map/while/body/eval_jaxpr/ppermute | solution.py:17
  178.9 1.5 pad_maximum_fusion.20
  183.9 6.8 %bitcast_dynamic-update-slice_fusion.2 = (bf16[4,16,8,8,384]{4,3,2,1,0:T(8,128)(2,1)}, f32[16,8,8,384]{3,2,1,0:T(8,128)S(1)}) fusion(bf16[4,16,8,8,384]{4,3,2,1,0:T(8,128)(2,1)} %get-tuple-element.177, s32[]{:T(128)S(6)} %copy.53, f32[16,8,8,384]{3,2,1,0:T(8,128)S(1)} %get-tuple-element.176, ...), kind=kOutput, calls=%fused_computation.52.clone.1 | convolution fusion | flops 2720268288 | bytes 16809988 | tf_op jit(solution)/shard_map/while/body/eval_jaxpr/...k,kg->...g/dot_general | solution.py:27
  190.9 3.7 %collective-permute-start = (bf16[16,1,8,384]{3,2,1,0:T(8,128)(2,1)S(1)}, bf16[16,1,8,384]{3,2,1,0:T(8,128)(2,1)S(1)}, u32[]{:S(2)}, u32[]{:S(2)}) collective-permute-start(bf16[16,1,8,384]{3,2,1,0:T(8,128)(2,1)S(1)} %get-tuple-element.152), channel_id=1, source_target_pairs={{1,0},{3,2},{5,4},{7,6},{9,8},{11,10},{13,12},{15,14},{17,16},{19,... | collective-permute-start | bytes 294920 | tf_op jit(solution)/shard_map/while/body/eval_jaxpr/ppermute | solution.py:13
  200.5 1.9 collective-permute-start.2
  202.5 3.4 collective-permute-start.3
  205.9 9.5 %fusion.51 = f32[16,8,8,1152]{3,2,1,0:T(8,128)S(1)} fusion(bf16[16,8,8,3456]{3,2,1,0:T(8,128)(2,1)S(1)} %slice_dynamic-update-slice_fusion.50, bf16[3456,1152]{1,0:T(8,128)(2,1)S(1)} %bitcast.61, f32[1152]{0:T(1024)S(1)} %get-tuple-element.189), kind=kOutput, calls=%fused_computation.4.clone.1 | convolution fusion | flops 8154906624 | bytes 19763712 | tf_op jit(solution)/shard_map/while/body/eval_jaxpr/...k,kg->...g/dot_general | solution.py:27
  215.4 1.5 pad_maximum_fusion.18
  219.8 6.1 %fusion.55 = f32[16,8,8,768]{3,2,1,0:T(8,128)S(1)} fusion(f32[16,8,8,1152]{3,2,1,0:T(8,128)S(1)} %fusion.51, bf16[16,8,8,3456]{3,2,1,0:T(8,128)(2,1)S(1)} %slice_dynamic-update-slice_fusion.56, bf16[3456,768]{1,0:T(8,128)(2,1)S(1)} %bitcast.64), kind=kOutput, calls=%fused_computation.9.clone.1 | convolution fusion | flops 5438963712 | bytes 18677760 | tf_op jit(solution)/shard_map/while/body/eval_jaxpr/...k,kg->...g/dot_general | solution.py:27
  226.3 4.0 %collective-permute-start.4 = (bf16[16,1,8,384]{3,2,1,0:T(8,128)(2,1)S(1)}, bf16[16,1,8,384]{3,2,1,0:T(8,128)(2,1)S(1)}, u32[]{:S(2)}, u32[]{:S(2)}) collective-permute-start(bf16[16,1,8,384]{3,2,1,0:T(8,128)(2,1)S(1)} %get-tuple-element.158), channel_id=1, source_target_pairs={{1,0},{3,2},{5,4},{7,6},{9,8},{11,10},{13,12},{15,14},{17,16},{19,... | collective-permute-start | bytes 294920 | tf_op jit(solution)/shard_map/while/body/eval_jaxpr/ppermute | solution.py:13
  231.6 1.9 collective-permute-done.5
  233.8 5.4 %collective-permute-start.6 = (bf16[16,10,1,384]{3,2,1,0:T(2,128)(2,1)S(1)}, bf16[16,10,1,384]{3,2,1,0:T(2,128)(2,1)S(1)}, u32[]{:S(2)}, u32[]{:S(2)}) collective-permute-start(bf16[16,10,1,384]{3,2,1,0:T(2,128)(2,1)S(1)} %get-tuple-element.160), channel_id=1, source_target_pairs={{2,0},{4,2},{6,4},{8,6},{10,8},{12,10},{14,12},{16,14},{18,16},{20... | collective-permute-start | bytes 368648 | tf_op jit(solution)/shard_map/while/body/eval_jaxpr/ppermute | solution.py:18
  239.3 1.9 collective-permute-start.7
  241.2 3.2 collective-permute-done.6
  244.4 8.1 %collective-permute-done.7 = bf16[16,10,1,384]{3,2,1,0:T(2,128)(2,1)S(1)} collective-permute-done((bf16[16,10,1,384]{3,2,1,0:T(2,128)(2,1)S(1)}, bf16[16,10,1,384]{3,2,1,0:T(2,128)(2,1)S(1)}, u32[]{:S(2)}, u32[]{:S(2)}) %collective-permute-start.7) | collective-permute-done | bytes 122912 | tf_op jit(solution)/shard_map/while/body/eval_jaxpr/ppermute | solution.py:17
  252.5 1.5 pad_maximum_fusion.20
  257.5 6.8 %bitcast_dynamic-update-slice_fusion.2 = (bf16[4,16,8,8,384]{4,3,2,1,0:T(8,128)(2,1)}, f32[16,8,8,384]{3,2,1,0:T(8,128)S(1)}) fusion(bf16[4,16,8,8,384]{4,3,2,1,0:T(8,128)(2,1)} %get-tuple-element.177, s32[]{:T(128)S(6)} %copy.53, f32[16,8,8,384]{3,2,1,0:T(8,128)S(1)} %get-tuple-element.176, ...), kind=kOutput, calls=%fused_computation.52.clone.1 | convolution fusion | flops 2720268288 | bytes 16809988 | tf_op jit(solution)/shard_map/while/body/eval_jaxpr/...k,kg->...g/dot_general | solution.py:27
  264.5 3.7 %collective-permute-start = (bf16[16,1,8,384]{3,2,1,0:T(8,128)(2,1)S(1)}, bf16[16,1,8,384]{3,2,1,0:T(8,128)(2,1)S(1)}, u32[]{:S(2)}, u32[]{:S(2)}) collective-permute-start(bf16[16,1,8,384]{3,2,1,0:T(8,128)(2,1)S(1)} %get-tuple-element.152), channel_id=1, source_target_pairs={{1,0},{3,2},{5,4},{7,6},{9,8},{11,10},{13,12},{15,14},{17,16},{19,... | collective-permute-start | bytes 294920 | tf_op jit(solution)/shard_map/while/body/eval_jaxpr/ppermute | solution.py:13
  274.1 1.9 collective-permute-start.2
  276.0 3.4 collective-permute-start.3
  279.4 9.5 %fusion.51 = f32[16,8,8,1152]{3,2,1,0:T(8,128)S(1)} fusion(bf16[16,8,8,3456]{3,2,1,0:T(8,128)(2,1)S(1)} %slice_dynamic-update-slice_fusion.50, bf16[3456,1152]{1,0:T(8,128)(2,1)S(1)} %bitcast.61, f32[1152]{0:T(1024)S(1)} %get-tuple-element.189), kind=kOutput, calls=%fused_computation.4.clone.1 | convolution fusion | flops 8154906624 | bytes 19763712 | tf_op jit(solution)/shard_map/while/body/eval_jaxpr/...k,kg->...g/dot_general | solution.py:27
  289.0 1.5 pad_maximum_fusion.18
  293.4 6.1 %fusion.55 = f32[16,8,8,768]{3,2,1,0:T(8,128)S(1)} fusion(f32[16,8,8,1152]{3,2,1,0:T(8,128)S(1)} %fusion.51, bf16[16,8,8,3456]{3,2,1,0:T(8,128)(2,1)S(1)} %slice_dynamic-update-slice_fusion.56, bf16[3456,768]{1,0:T(8,128)(2,1)S(1)} %bitcast.64), kind=kOutput, calls=%fused_computation.9.clone.1 | convolution fusion | flops 5438963712 | bytes 18677760 | tf_op jit(solution)/shard_map/while/body/eval_jaxpr/...k,kg->...g/dot_general | solution.py:27
  299.8 4.0 %collective-permute-start.4 = (bf16[16,1,8,384]{3,2,1,0:T(8,128)(2,1)S(1)}, bf16[16,1,8,384]{3,2,1,0:T(8,128)(2,1)S(1)}, u32[]{:S(2)}, u32[]{:S(2)}) collective-permute-start(bf16[16,1,8,384]{3,2,1,0:T(8,128)(2,1)S(1)} %get-tuple-element.158), channel_id=1, source_target_pairs={{1,0},{3,2},{5,4},{7,6},{9,8},{11,10},{13,12},{15,14},{17,16},{19,... | collective-permute-start | bytes 294920 | tf_op jit(solution)/shard_map/while/body/eval_jaxpr/ppermute | solution.py:13
  305.2 1.9 collective-permute-done.5
  307.4 5.4 %collective-permute-start.6 = (bf16[16,10,1,384]{3,2,1,0:T(2,128)(2,1)S(1)}, bf16[16,10,1,384]{3,2,1,0:T(2,128)(2,1)S(1)}, u32[]{:S(2)}, u32[]{:S(2)}) collective-permute-start(bf16[16,10,1,384]{3,2,1,0:T(2,128)(2,1)S(1)} %get-tuple-element.160), channel_id=1, source_target_pairs={{2,0},{4,2},{6,4},{8,6},{10,8},{12,10},{14,12},{16,14},{18,16},{20... | collective-permute-start | bytes 368648 | tf_op jit(solution)/shard_map/while/body/eval_jaxpr/ppermute | solution.py:18
  312.8 1.9 collective-permute-start.7
  314.7 3.2 collective-permute-done.6
  317.9 8.1 %collective-permute-done.7 = bf16[16,10,1,384]{3,2,1,0:T(2,128)(2,1)S(1)} collective-permute-done((bf16[16,10,1,384]{3,2,1,0:T(2,128)(2,1)S(1)}, bf16[16,10,1,384]{3,2,1,0:T(2,128)(2,1)S(1)}, u32[]{:S(2)}, u32[]{:S(2)}) %collective-permute-start.7) | collective-permute-done | bytes 122912 | tf_op jit(solution)/shard_map/while/body/eval_jaxpr/ppermute | solution.py:17
  326.0 1.5 pad_maximum_fusion.20
  331.1 6.8 %bitcast_dynamic-update-slice_fusion.2 = (bf16[4,16,8,8,384]{4,3,2,1,0:T(8,128)(2,1)}, f32[16,8,8,384]{3,2,1,0:T(8,128)S(1)}) fusion(bf16[4,16,8,8,384]{4,3,2,1,0:T(8,128)(2,1)} %get-tuple-element.177, s32[]{:T(128)S(6)} %copy.53, f32[16,8,8,384]{3,2,1,0:T(8,128)S(1)} %get-tuple-element.176, ...), kind=kOutput, calls=%fused_computation.52.clone.1 | convolution fusion | flops 2720268288 | bytes 16809988 | tf_op jit(solution)/shard_map/while/body/eval_jaxpr/...k,kg->...g/dot_general | solution.py:27
  (260 shorter events, 62.9 us)
Async XLA Ops:
  0.6 5.9 %copy-start.5 = (bf16[4,16,8,8,384]{4,3,2,1,0:T(8,128)(2,1)S(1)}, bf16[4,16,8,8,384]{4,3,2,1,0:T(8,128)(2,1)}, u32[]{:S(2)}) copy-start(bf16[4,16,8,8,384]{4,3,2,1,0:T(8,128)(2,1)} %param.8) | copy-start | bytes 9437188
  2.0 4.4 %collective-permute-start.8 = (bf16[4,16,1,8,384]{4,1,3,2,0:T(8,128)(2,1)S(1)}, bf16[4,16,1,8,384]{4,1,3,2,0:T(8,128)(2,1)S(1)}, u32[]{:S(2)}, u32[]{:S(2)}) collective-permute-start(bf16[4,16,1,8,384]{4,1,3,2,0:T(8,128)(2,1)S(1)} %copy.18), channel_id=1, source_target_pairs={{0,1},{2,3},{4,5},{6,7},{8,9},{10,11},{12,13},{14,15},{16,17},{18,... | collective-permute-start | bytes 1179656 | tf_op jit(solution)/shard_map/ppermute | solution.py:12
  3.4 6.4 %collective-permute-start.9 = (bf16[4,16,1,8,384]{4,1,3,2,0:T(8,128)(2,1)S(1)}, bf16[4,16,1,8,384]{4,1,3,2,0:T(8,128)(2,1)S(1)}, u32[]{:S(2)}, u32[]{:S(2)}) collective-permute-start(bf16[4,16,1,8,384]{4,1,3,2,0:T(8,128)(2,1)S(1)} %copy.19), channel_id=1, source_target_pairs={{1,0},{3,2},{5,4},{7,6},{9,8},{11,10},{13,12},{15,14},{17,16},{19,... | collective-permute-start | bytes 1179656 | tf_op jit(solution)/shard_map/ppermute | solution.py:13
  12.7 19.1 %collective-permute-start.10 = (bf16[4,16,10,1,384]{4,1,3,2,0:T(8,128)(2,1)}, bf16[4,16,10,1,384]{4,1,3,2,0:T(8,128)(2,1)S(1)}, u32[]{:S(2)}, u32[]{:S(2)}) collective-permute-start(bf16[4,16,10,1,384]{4,1,3,2,0:T(8,128)(2,1)} %get-tuple-element.85), channel_id=1, source_target_pairs={{0,2},{2,4},{4,6},{6,8},{8,10},{10,12},{12,14},{14,16},{16,18},{18... | collective-permute-start | bytes 1474568 | tf_op jit(solution)/shard_map/ppermute | solution.py:17
  15.8 17.3 %collective-permute-start.11 = (bf16[4,16,10,1,384]{4,1,3,2,0:T(8,128)(2,1)S(1)}, bf16[4,16,10,1,384]{4,1,3,2,0:T(8,128)(2,1)S(1)}, u32[]{:S(2)}, u32[]{:S(2)}) collective-permute-start(bf16[4,16,10,1,384]{4,1,3,2,0:T(8,128)(2,1)S(1)} %get-tuple-element.86), channel_id=1, source_target_pairs={{2,0},{4,2},{6,4},{8,6},{10,8},{12,10},{14,12},{16,14},{18,16},{20... | collective-permute-start | bytes 1474568 | tf_op jit(solution)/shard_map/ppermute | solution.py:18
  22.2 15.9 %copy-start.1 = (f32[16,8,8,384]{3,2,1,0:T(8,128)S(1)}, f32[16,8,8,384]{3,2,1,0:T(8,128)}, u32[]{:S(2)}) copy-start(f32[16,8,8,384]{3,2,1,0:T(8,128)} %param.9) | copy-start | bytes 4718596
  22.2 15.9 %copy-start.7 = (f32[1152]{0:T(1024)S(1)}, f32[1152]{0:T(1024)}, u32[]{:S(2)}) copy-start(f32[1152]{0:T(1024)} %param.13) | copy-start | bytes 13828
  38.3 8.1 %collective-permute-start = (bf16[16,1,8,384]{3,2,1,0:T(8,128)(2,1)S(1)}, bf16[16,1,8,384]{3,2,1,0:T(8,128)(2,1)S(1)}, u32[]{:S(2)}, u32[]{:S(2)}) collective-permute-start(bf16[16,1,8,384]{3,2,1,0:T(8,128)(2,1)S(1)} %get-tuple-element.152), channel_id=1, source_target_pairs={{1,0},{3,2},{5,4},{7,6},{9,8},{11,10},{13,12},{15,14},{17,16},{19,... | collective-permute-start | bytes 294920 | tf_op jit(solution)/shard_map/while/body/eval_jaxpr/ppermute | solution.py:13
  40.8 5.5 %collective-permute-start.1 = (bf16[16,1,8,384]{3,2,1,0:T(8,128)(2,1)S(1)}, bf16[16,1,8,384]{3,2,1,0:T(8,128)(2,1)S(1)}, u32[]{:S(2)}, u32[]{:S(2)}) collective-permute-start(bf16[16,1,8,384]{3,2,1,0:T(8,128)(2,1)S(1)} %get-tuple-element.153), channel_id=1, source_target_pairs={{0,1},{2,3},{4,5},{6,7},{8,9},{10,11},{12,13},{14,15},{16,17},{18,... | collective-permute-start | bytes 294920 | tf_op jit(solution)/shard_map/while/body/eval_jaxpr/ppermute | solution.py:12
  43.9 13.1 %slice-start = ((s8[7962624]{0:T(1024)(128)(4,1)}), s8[4194304]{0:T(1024)(128)(4,1)S(1)}, s32[]{:S(2)}) async-start(s8[7962624]{0:T(1024)(128)(4,1)} %bitcast.60), calls=%async_computation | async-start | bytes 8388608 | tf_op jit(solution)/shard_map/while
  44.9 12.1 %slice-start.1 = ((s8[7962624]{0:T(1024)(128)(4,1)}), s8[3768320]{0:T(1024)(128)(4,1)S(1)}, s32[]{:S(2)}) async-start(s8[7962624]{0:T(1024)(128)(4,1)} %bitcast.60), calls=%async_computation.1 | async-start | bytes 7536640 | tf_op jit(solution)/shard_map/while
  46.7 19.9 %collective-permute-start.2 = (bf16[16,10,1,384]{3,2,1,0:T(2,128)(2,1)S(1)}, bf16[16,10,1,384]{3,2,1,0:T(2,128)(2,1)S(1)}, u32[]{:S(2)}, u32[]{:S(2)}) collective-permute-start(bf16[16,10,1,384]{3,2,1,0:T(2,128)(2,1)S(1)} %get-tuple-element.154), channel_id=1, source_target_pairs={{2,0},{4,2},{6,4},{8,6},{10,8},{12,10},{14,12},{16,14},{18,16},{20... | collective-permute-start | bytes 368648 | tf_op jit(solution)/shard_map/while/body/eval_jaxpr/ppermute | solution.py:18
  55.1 12.2 %collective-permute-start.3 = (bf16[16,10,1,384]{3,2,1,0:T(2,128)(2,1)S(1)}, bf16[16,10,1,384]{3,2,1,0:T(2,128)(2,1)S(1)}, u32[]{:S(2)}, u32[]{:S(2)}) collective-permute-start(bf16[16,10,1,384]{3,2,1,0:T(2,128)(2,1)S(1)} %get-tuple-element.155), channel_id=1, source_target_pairs={{0,2},{2,4},{4,6},{6,8},{8,10},{10,12},{12,14},{14,16},{16,18},{18... | collective-permute-start | bytes 368648 | tf_op jit(solution)/shard_map/while/body/eval_jaxpr/ppermute | solution.py:17
  66.6 4.3 %copy-start.8 = (f32[16,8,8,1152]{3,2,1,0:T(8,128)}, f32[16,8,8,1152]{3,2,1,0:T(8,128)S(1)}, u32[]{:S(2)}) copy-start(f32[16,8,8,1152]{3,2,1,0:T(8,128)S(1)} %fusion.51) | copy-start | bytes 14155780 | tf_op jit(solution)/shard_map/while
  68.9 2.2 slice-start.2
  69.6 2.0 slice-start.3
  77.8 8.4 %copy-start.2 = (f32[16,8,8,768]{3,2,1,0:T(8,128)}, f32[16,8,8,768]{3,2,1,0:T(8,128)S(1)}, u32[]{:S(2)}) copy-start(f32[16,8,8,768]{3,2,1,0:T(8,128)S(1)} %fusion.55) | copy-start | bytes 9437188 | tf_op jit(solution)/shard_map/while
  78.1 6.2 %collective-permute-start.4 = (bf16[16,1,8,384]{3,2,1,0:T(8,128)(2,1)S(1)}, bf16[16,1,8,384]{3,2,1,0:T(8,128)(2,1)S(1)}, u32[]{:S(2)}, u32[]{:S(2)}) collective-permute-start(bf16[16,1,8,384]{3,2,1,0:T(8,128)(2,1)S(1)} %get-tuple-element.158), channel_id=1, source_target_pairs={{1,0},{3,2},{5,4},{7,6},{9,8},{11,10},{13,12},{15,14},{17,16},{19,... | collective-permute-start | bytes 294920 | tf_op jit(solution)/shard_map/while/body/eval_jaxpr/ppermute | solution.py:13
  83.0 3.2 collective-permute-start.5
  86.5 10.8 %collective-permute-start.6 = (bf16[16,10,1,384]{3,2,1,0:T(2,128)(2,1)S(1)}, bf16[16,10,1,384]{3,2,1,0:T(2,128)(2,1)S(1)}, u32[]{:S(2)}, u32[]{:S(2)}) collective-permute-start(bf16[16,10,1,384]{3,2,1,0:T(2,128)(2,1)S(1)} %get-tuple-element.160), channel_id=1, source_target_pairs={{2,0},{4,2},{6,4},{8,6},{10,8},{12,10},{14,12},{16,14},{18,16},{20... | collective-permute-start | bytes 368648 | tf_op jit(solution)/shard_map/while/body/eval_jaxpr/ppermute | solution.py:18
  92.1 13.2 %collective-permute-start.7 = (bf16[16,10,1,384]{3,2,1,0:T(2,128)(2,1)S(1)}, bf16[16,10,1,384]{3,2,1,0:T(2,128)(2,1)S(1)}, u32[]{:S(2)}, u32[]{:S(2)}) collective-permute-start(bf16[16,10,1,384]{3,2,1,0:T(2,128)(2,1)S(1)} %get-tuple-element.161), channel_id=1, source_target_pairs={{0,2},{2,4},{4,6},{6,8},{8,10},{10,12},{12,14},{14,16},{16,18},{18... | collective-permute-start | bytes 368648 | tf_op jit(solution)/shard_map/while/body/eval_jaxpr/ppermute | solution.py:17
  107.7 2.7 copy-start.6
  117.3 9.3 %collective-permute-start = (bf16[16,1,8,384]{3,2,1,0:T(8,128)(2,1)S(1)}, bf16[16,1,8,384]{3,2,1,0:T(8,128)(2,1)S(1)}, u32[]{:S(2)}, u32[]{:S(2)}) collective-permute-start(bf16[16,1,8,384]{3,2,1,0:T(8,128)(2,1)S(1)} %get-tuple-element.152), channel_id=1, source_target_pairs={{1,0},{3,2},{5,4},{7,6},{9,8},{11,10},{13,12},{15,14},{17,16},{19,... | collective-permute-start | bytes 294920 | tf_op jit(solution)/shard_map/while/body/eval_jaxpr/ppermute | solution.py:13
  121.1 5.5 %collective-permute-start.1 = (bf16[16,1,8,384]{3,2,1,0:T(8,128)(2,1)S(1)}, bf16[16,1,8,384]{3,2,1,0:T(8,128)(2,1)S(1)}, u32[]{:S(2)}, u32[]{:S(2)}) collective-permute-start(bf16[16,1,8,384]{3,2,1,0:T(8,128)(2,1)S(1)} %get-tuple-element.153), channel_id=1, source_target_pairs={{0,1},{2,3},{4,5},{6,7},{8,9},{10,11},{12,13},{14,15},{16,17},{18,... | collective-permute-start | bytes 294920 | tf_op jit(solution)/shard_map/while/body/eval_jaxpr/ppermute | solution.py:12
  124.2 8.1 %slice-start = ((s8[7962624]{0:T(1024)(128)(4,1)}), s8[4194304]{0:T(1024)(128)(4,1)S(1)}, s32[]{:S(2)}) async-start(s8[7962624]{0:T(1024)(128)(4,1)} %bitcast.60), calls=%async_computation | async-start | bytes 8388608 | tf_op jit(solution)/shard_map/while
  125.2 7.1 %slice-start.1 = ((s8[7962624]{0:T(1024)(128)(4,1)}), s8[3768320]{0:T(1024)(128)(4,1)S(1)}, s32[]{:S(2)}) async-start(s8[7962624]{0:T(1024)(128)(4,1)} %bitcast.60), calls=%async_computation.1 | async-start | bytes 7536640 | tf_op jit(solution)/shard_map/while
  127.0 14.9 %collective-permute-start.2 = (bf16[16,10,1,384]{3,2,1,0:T(2,128)(2,1)S(1)}, bf16[16,10,1,384]{3,2,1,0:T(2,128)(2,1)S(1)}, u32[]{:S(2)}, u32[]{:S(2)}) collective-permute-start(bf16[16,10,1,384]{3,2,1,0:T(2,128)(2,1)S(1)} %get-tuple-element.154), channel_id=1, source_target_pairs={{2,0},{4,2},{6,4},{8,6},{10,8},{12,10},{14,12},{16,14},{18,16},{20... | collective-permute-start | bytes 368648 | tf_op jit(solution)/shard_map/while/body/eval_jaxpr/ppermute | solution.py:18
  128.9 13.0 %collective-permute-start.3 = (bf16[16,10,1,384]{3,2,1,0:T(2,128)(2,1)S(1)}, bf16[16,10,1,384]{3,2,1,0:T(2,128)(2,1)S(1)}, u32[]{:S(2)}, u32[]{:S(2)}) collective-permute-start(bf16[16,10,1,384]{3,2,1,0:T(2,128)(2,1)S(1)} %get-tuple-element.155), channel_id=1, source_target_pairs={{0,2},{2,4},{4,6},{6,8},{8,10},{10,12},{12,14},{14,16},{16,18},{18... | collective-permute-start | bytes 368648 | tf_op jit(solution)/shard_map/while/body/eval_jaxpr/ppermute | solution.py:17
  141.8 3.6 %copy-start.8 = (f32[16,8,8,1152]{3,2,1,0:T(8,128)}, f32[16,8,8,1152]{3,2,1,0:T(8,128)S(1)}, u32[]{:S(2)}) copy-start(f32[16,8,8,1152]{3,2,1,0:T(8,128)S(1)} %fusion.51) | copy-start | bytes 14155780 | tf_op jit(solution)/shard_map/while
  143.6 2.2 slice-start.2
  152.4 7.6 %copy-start.2 = (f32[16,8,8,768]{3,2,1,0:T(8,128)}, f32[16,8,8,768]{3,2,1,0:T(8,128)S(1)}, u32[]{:S(2)}) copy-start(f32[16,8,8,768]{3,2,1,0:T(8,128)S(1)} %fusion.55) | copy-start | bytes 9437188 | tf_op jit(solution)/shard_map/while
  152.7 5.3 %collective-permute-start.4 = (bf16[16,1,8,384]{3,2,1,0:T(8,128)(2,1)S(1)}, bf16[16,1,8,384]{3,2,1,0:T(8,128)(2,1)S(1)}, u32[]{:S(2)}, u32[]{:S(2)}) collective-permute-start(bf16[16,1,8,384]{3,2,1,0:T(8,128)(2,1)S(1)} %get-tuple-element.158), channel_id=1, source_target_pairs={{1,0},{3,2},{5,4},{7,6},{9,8},{11,10},{13,12},{15,14},{17,16},{19,... | collective-permute-start | bytes 294920 | tf_op jit(solution)/shard_map/while/body/eval_jaxpr/ppermute | solution.py:13
  156.7 3.2 collective-permute-start.5
  160.3 10.6 %collective-permute-start.6 = (bf16[16,10,1,384]{3,2,1,0:T(2,128)(2,1)S(1)}, bf16[16,10,1,384]{3,2,1,0:T(2,128)(2,1)S(1)}, u32[]{:S(2)}, u32[]{:S(2)}) collective-permute-start(bf16[16,10,1,384]{3,2,1,0:T(2,128)(2,1)S(1)} %get-tuple-element.160), channel_id=1, source_target_pairs={{2,0},{4,2},{6,4},{8,6},{10,8},{12,10},{14,12},{16,14},{18,16},{20... | collective-permute-start | bytes 368648 | tf_op jit(solution)/shard_map/while/body/eval_jaxpr/ppermute | solution.py:18
  165.7 13.2 %collective-permute-start.7 = (bf16[16,10,1,384]{3,2,1,0:T(2,128)(2,1)S(1)}, bf16[16,10,1,384]{3,2,1,0:T(2,128)(2,1)S(1)}, u32[]{:S(2)}, u32[]{:S(2)}) collective-permute-start(bf16[16,10,1,384]{3,2,1,0:T(2,128)(2,1)S(1)} %get-tuple-element.161), channel_id=1, source_target_pairs={{0,2},{2,4},{4,6},{6,8},{8,10},{10,12},{12,14},{14,16},{16,18},{18... | collective-permute-start | bytes 368648 | tf_op jit(solution)/shard_map/while/body/eval_jaxpr/ppermute | solution.py:17
  181.2 2.7 copy-start.6
  190.9 9.3 %collective-permute-start = (bf16[16,1,8,384]{3,2,1,0:T(8,128)(2,1)S(1)}, bf16[16,1,8,384]{3,2,1,0:T(8,128)(2,1)S(1)}, u32[]{:S(2)}, u32[]{:S(2)}) collective-permute-start(bf16[16,1,8,384]{3,2,1,0:T(8,128)(2,1)S(1)} %get-tuple-element.152), channel_id=1, source_target_pairs={{1,0},{3,2},{5,4},{7,6},{9,8},{11,10},{13,12},{15,14},{17,16},{19,... | collective-permute-start | bytes 294920 | tf_op jit(solution)/shard_map/while/body/eval_jaxpr/ppermute | solution.py:13
  194.6 5.5 %collective-permute-start.1 = (bf16[16,1,8,384]{3,2,1,0:T(8,128)(2,1)S(1)}, bf16[16,1,8,384]{3,2,1,0:T(8,128)(2,1)S(1)}, u32[]{:S(2)}, u32[]{:S(2)}) collective-permute-start(bf16[16,1,8,384]{3,2,1,0:T(8,128)(2,1)S(1)} %get-tuple-element.153), channel_id=1, source_target_pairs={{0,1},{2,3},{4,5},{6,7},{8,9},{10,11},{12,13},{14,15},{16,17},{18,... | collective-permute-start | bytes 294920 | tf_op jit(solution)/shard_map/while/body/eval_jaxpr/ppermute | solution.py:12
  197.8 8.1 %slice-start = ((s8[7962624]{0:T(1024)(128)(4,1)}), s8[4194304]{0:T(1024)(128)(4,1)S(1)}, s32[]{:S(2)}) async-start(s8[7962624]{0:T(1024)(128)(4,1)} %bitcast.60), calls=%async_computation | async-start | bytes 8388608 | tf_op jit(solution)/shard_map/while
  198.7 7.1 %slice-start.1 = ((s8[7962624]{0:T(1024)(128)(4,1)}), s8[3768320]{0:T(1024)(128)(4,1)S(1)}, s32[]{:S(2)}) async-start(s8[7962624]{0:T(1024)(128)(4,1)} %bitcast.60), calls=%async_computation.1 | async-start | bytes 7536640 | tf_op jit(solution)/shard_map/while
  200.5 14.9 %collective-permute-start.2 = (bf16[16,10,1,384]{3,2,1,0:T(2,128)(2,1)S(1)}, bf16[16,10,1,384]{3,2,1,0:T(2,128)(2,1)S(1)}, u32[]{:S(2)}, u32[]{:S(2)}) collective-permute-start(bf16[16,10,1,384]{3,2,1,0:T(2,128)(2,1)S(1)} %get-tuple-element.154), channel_id=1, source_target_pairs={{2,0},{4,2},{6,4},{8,6},{10,8},{12,10},{14,12},{16,14},{18,16},{20... | collective-permute-start | bytes 368648 | tf_op jit(solution)/shard_map/while/body/eval_jaxpr/ppermute | solution.py:18
  202.5 13.0 %collective-permute-start.3 = (bf16[16,10,1,384]{3,2,1,0:T(2,128)(2,1)S(1)}, bf16[16,10,1,384]{3,2,1,0:T(2,128)(2,1)S(1)}, u32[]{:S(2)}, u32[]{:S(2)}) collective-permute-start(bf16[16,10,1,384]{3,2,1,0:T(2,128)(2,1)S(1)} %get-tuple-element.155), channel_id=1, source_target_pairs={{0,2},{2,4},{4,6},{6,8},{8,10},{10,12},{12,14},{14,16},{16,18},{18... | collective-permute-start | bytes 368648 | tf_op jit(solution)/shard_map/while/body/eval_jaxpr/ppermute | solution.py:17
  215.4 3.6 %copy-start.8 = (f32[16,8,8,1152]{3,2,1,0:T(8,128)}, f32[16,8,8,1152]{3,2,1,0:T(8,128)S(1)}, u32[]{:S(2)}) copy-start(f32[16,8,8,1152]{3,2,1,0:T(8,128)S(1)} %fusion.51) | copy-start | bytes 14155780 | tf_op jit(solution)/shard_map/while
  217.1 2.2 slice-start.2
  225.9 7.6 %copy-start.2 = (f32[16,8,8,768]{3,2,1,0:T(8,128)}, f32[16,8,8,768]{3,2,1,0:T(8,128)S(1)}, u32[]{:S(2)}) copy-start(f32[16,8,8,768]{3,2,1,0:T(8,128)S(1)} %fusion.55) | copy-start | bytes 9437188 | tf_op jit(solution)/shard_map/while
  226.3 5.3 %collective-permute-start.4 = (bf16[16,1,8,384]{3,2,1,0:T(8,128)(2,1)S(1)}, bf16[16,1,8,384]{3,2,1,0:T(8,128)(2,1)S(1)}, u32[]{:S(2)}, u32[]{:S(2)}) collective-permute-start(bf16[16,1,8,384]{3,2,1,0:T(8,128)(2,1)S(1)} %get-tuple-element.158), channel_id=1, source_target_pairs={{1,0},{3,2},{5,4},{7,6},{9,8},{11,10},{13,12},{15,14},{17,16},{19,... | collective-permute-start | bytes 294920 | tf_op jit(solution)/shard_map/while/body/eval_jaxpr/ppermute | solution.py:13
  230.3 3.2 collective-permute-start.5
  233.8 10.6 %collective-permute-start.6 = (bf16[16,10,1,384]{3,2,1,0:T(2,128)(2,1)S(1)}, bf16[16,10,1,384]{3,2,1,0:T(2,128)(2,1)S(1)}, u32[]{:S(2)}, u32[]{:S(2)}) collective-permute-start(bf16[16,10,1,384]{3,2,1,0:T(2,128)(2,1)S(1)} %get-tuple-element.160), channel_id=1, source_target_pairs={{2,0},{4,2},{6,4},{8,6},{10,8},{12,10},{14,12},{16,14},{18,16},{20... | collective-permute-start | bytes 368648 | tf_op jit(solution)/shard_map/while/body/eval_jaxpr/ppermute | solution.py:18
  239.3 13.2 %collective-permute-start.7 = (bf16[16,10,1,384]{3,2,1,0:T(2,128)(2,1)S(1)}, bf16[16,10,1,384]{3,2,1,0:T(2,128)(2,1)S(1)}, u32[]{:S(2)}, u32[]{:S(2)}) collective-permute-start(bf16[16,10,1,384]{3,2,1,0:T(2,128)(2,1)S(1)} %get-tuple-element.161), channel_id=1, source_target_pairs={{0,2},{2,4},{4,6},{6,8},{8,10},{10,12},{12,14},{14,16},{16,18},{18... | collective-permute-start | bytes 368648 | tf_op jit(solution)/shard_map/while/body/eval_jaxpr/ppermute | solution.py:17
  254.8 2.7 copy-start.6
  264.5 9.3 %collective-permute-start = (bf16[16,1,8,384]{3,2,1,0:T(8,128)(2,1)S(1)}, bf16[16,1,8,384]{3,2,1,0:T(8,128)(2,1)S(1)}, u32[]{:S(2)}, u32[]{:S(2)}) collective-permute-start(bf16[16,1,8,384]{3,2,1,0:T(8,128)(2,1)S(1)} %get-tuple-element.152), channel_id=1, source_target_pairs={{1,0},{3,2},{5,4},{7,6},{9,8},{11,10},{13,12},{15,14},{17,16},{19,... | collective-permute-start | bytes 294920 | tf_op jit(solution)/shard_map/while/body/eval_jaxpr/ppermute | solution.py:13
  268.2 5.5 %collective-permute-start.1 = (bf16[16,1,8,384]{3,2,1,0:T(8,128)(2,1)S(1)}, bf16[16,1,8,384]{3,2,1,0:T(8,128)(2,1)S(1)}, u32[]{:S(2)}, u32[]{:S(2)}) collective-permute-start(bf16[16,1,8,384]{3,2,1,0:T(8,128)(2,1)S(1)} %get-tuple-element.153), channel_id=1, source_target_pairs={{0,1},{2,3},{4,5},{6,7},{8,9},{10,11},{12,13},{14,15},{16,17},{18,... | collective-permute-start | bytes 294920 | tf_op jit(solution)/shard_map/while/body/eval_jaxpr/ppermute | solution.py:12
  271.3 8.1 %slice-start = ((s8[7962624]{0:T(1024)(128)(4,1)}), s8[4194304]{0:T(1024)(128)(4,1)S(1)}, s32[]{:S(2)}) async-start(s8[7962624]{0:T(1024)(128)(4,1)} %bitcast.60), calls=%async_computation | async-start | bytes 8388608 | tf_op jit(solution)/shard_map/while
  272.3 7.1 %slice-start.1 = ((s8[7962624]{0:T(1024)(128)(4,1)}), s8[3768320]{0:T(1024)(128)(4,1)S(1)}, s32[]{:S(2)}) async-start(s8[7962624]{0:T(1024)(128)(4,1)} %bitcast.60), calls=%async_computation.1 | async-start | bytes 7536640 | tf_op jit(solution)/shard_map/while
  274.1 14.9 %collective-permute-start.2 = (bf16[16,10,1,384]{3,2,1,0:T(2,128)(2,1)S(1)}, bf16[16,10,1,384]{3,2,1,0:T(2,128)(2,1)S(1)}, u32[]{:S(2)}, u32[]{:S(2)}) collective-permute-start(bf16[16,10,1,384]{3,2,1,0:T(2,128)(2,1)S(1)} %get-tuple-element.154), channel_id=1, source_target_pairs={{2,0},{4,2},{6,4},{8,6},{10,8},{12,10},{14,12},{16,14},{18,16},{20... | collective-permute-start | bytes 368648 | tf_op jit(solution)/shard_map/while/body/eval_jaxpr/ppermute | solution.py:18
  276.0 13.0 %collective-permute-start.3 = (bf16[16,10,1,384]{3,2,1,0:T(2,128)(2,1)S(1)}, bf16[16,10,1,384]{3,2,1,0:T(2,128)(2,1)S(1)}, u32[]{:S(2)}, u32[]{:S(2)}) collective-permute-start(bf16[16,10,1,384]{3,2,1,0:T(2,128)(2,1)S(1)} %get-tuple-element.155), channel_id=1, source_target_pairs={{0,2},{2,4},{4,6},{6,8},{8,10},{10,12},{12,14},{14,16},{16,18},{18... | collective-permute-start | bytes 368648 | tf_op jit(solution)/shard_map/while/body/eval_jaxpr/ppermute | solution.py:17
  289.0 3.6 %copy-start.8 = (f32[16,8,8,1152]{3,2,1,0:T(8,128)}, f32[16,8,8,1152]{3,2,1,0:T(8,128)S(1)}, u32[]{:S(2)}) copy-start(f32[16,8,8,1152]{3,2,1,0:T(8,128)S(1)} %fusion.51) | copy-start | bytes 14155780 | tf_op jit(solution)/shard_map/while
  290.7 2.2 slice-start.2
  299.5 7.6 %copy-start.2 = (f32[16,8,8,768]{3,2,1,0:T(8,128)}, f32[16,8,8,768]{3,2,1,0:T(8,128)S(1)}, u32[]{:S(2)}) copy-start(f32[16,8,8,768]{3,2,1,0:T(8,128)S(1)} %fusion.55) | copy-start | bytes 9437188 | tf_op jit(solution)/shard_map/while
  299.8 5.3 %collective-permute-start.4 = (bf16[16,1,8,384]{3,2,1,0:T(8,128)(2,1)S(1)}, bf16[16,1,8,384]{3,2,1,0:T(8,128)(2,1)S(1)}, u32[]{:S(2)}, u32[]{:S(2)}) collective-permute-start(bf16[16,1,8,384]{3,2,1,0:T(8,128)(2,1)S(1)} %get-tuple-element.158), channel_id=1, source_target_pairs={{1,0},{3,2},{5,4},{7,6},{9,8},{11,10},{13,12},{15,14},{17,16},{19,... | collective-permute-start | bytes 294920 | tf_op jit(solution)/shard_map/while/body/eval_jaxpr/ppermute | solution.py:13
  303.9 3.2 collective-permute-start.5
  307.4 10.6 %collective-permute-start.6 = (bf16[16,10,1,384]{3,2,1,0:T(2,128)(2,1)S(1)}, bf16[16,10,1,384]{3,2,1,0:T(2,128)(2,1)S(1)}, u32[]{:S(2)}, u32[]{:S(2)}) collective-permute-start(bf16[16,10,1,384]{3,2,1,0:T(2,128)(2,1)S(1)} %get-tuple-element.160), channel_id=1, source_target_pairs={{2,0},{4,2},{6,4},{8,6},{10,8},{12,10},{14,12},{16,14},{18,16},{20... | collective-permute-start | bytes 368648 | tf_op jit(solution)/shard_map/while/body/eval_jaxpr/ppermute | solution.py:18
  312.8 13.2 %collective-permute-start.7 = (bf16[16,10,1,384]{3,2,1,0:T(2,128)(2,1)S(1)}, bf16[16,10,1,384]{3,2,1,0:T(2,128)(2,1)S(1)}, u32[]{:S(2)}, u32[]{:S(2)}) collective-permute-start(bf16[16,10,1,384]{3,2,1,0:T(2,128)(2,1)S(1)} %get-tuple-element.161), channel_id=1, source_target_pairs={{0,2},{2,4},{4,6},{6,8},{8,10},{10,12},{12,14},{14,16},{16,18},{18... | collective-permute-start | bytes 368648 | tf_op jit(solution)/shard_map/while/body/eval_jaxpr/ppermute | solution.py:17
  328.4 2.7 copy-start.6
  (9 other events, 16.6 us)
where the time goes:
time: 341 us; the launch traced here: 339 us
  starting transfers between devices  111 us (33%)
  matrix products  90 us (26%)
  waiting for transfers between devices  64.2 us (19%)
  local copies, waits for them, and re-layouts  47 us (14%)
  other arithmetic  24.6 us (7%)
    dot_general x12, matrix products, im2col_conv(): jnp.einsum('...k,kg->...g', patches, w_mat, preferred_element_type=jnp.fl...  90 us
    ppermute x9, waiting for transfers between devices, with_halo(): lax.ppermute(tall_tile[..., tile_w - width:, :], 'cols', right_pairs)  42.5 us
    ppermute x9, starting transfers between devices, with_halo(): from_right = lax.ppermute(tall_tile[..., :width, :], 'cols', left_pairs)  42.4 us
    ppermute x9, starting transfers between devices, with_halo(): from_below = lax.ppermute(tile[..., :width, :, :], 'rows', up_pairs)  33.7 us
    while x140, local copies, waits for them, and re-layouts  27 us
    ppermute x9, starting transfers between devices, with_halo(): lax.ppermute(tall_tile[..., tile_w - width:, :], 'cols', right_pairs)  22.8 us
    concatenate x9, other arithmetic, with_halo(): return jnp.concatenate([from_left, tall_tile, from_right], axis=-2)  17.3 us
    ppermute x9, waiting for transfers between devices, with_halo(): from_right = lax.ppermute(tall_tile[..., :width, :], 'cols', left_pairs)  14.1 us
  transfers between devices with their start and end apart: 36, of which 15 were waited for; matrix products, arithmetic and copies ran while one was open for 17% of the time, Pallas kernels for 0%

commit v1 on v0

v1 whole, which is shorter than its diff:
```python
import jax
import jax.numpy as jnp
from jax import lax
from jax.experimental import pallas as pl
from jax.experimental.pallas import tpu as pltpu
from jax.sharding import PartitionSpec as P

MESH = pl.DeviceIdType.MESH
BF = jnp.bfloat16
F32 = jnp.float32
L = 128


def sigmoid(v):
    return 0.5 * jnp.tanh(0.5 * v) + 0.5


def make_kernel(steps, tile_h, tile_w, batch, ch, n_cols):
    half_w = tile_w // 2

    def kernel(frames, h0, wx, wz, wn, bias, h_seq, h_last,
               xb, hb, rb, hf, zf, gv, wxv, wzv, wnv, send_sem, recv_sem, load_sem, out_sem):
        row = lax.axis_index('rows')
        col = lax.axis_index('cols')
        has_left = col > 0
        has_right = col < n_cols - 1
        left, right, other = col - 1, col + 1, 1 - row
        src_row = tile_h - (tile_h - 1) * row
        dst_row = (tile_h + 1) * row

        inner = (pl.ds(1, tile_h), pl.ds(1, tile_w))

        def load_frame(t):
            return pltpu.make_async_copy(frames.at[t], xb.at[(t,) + inner], load_sem.at[t])

        def load_w(src, dst, first, width, sem):
            return pltpu.make_async_copy(src.at[:, pl.ds(first, width)], dst.at[:, pl.ds(first, width)], load_sem.at[sem])

        load_h = pltpu.make_async_copy(h0, hf, load_sem.at[steps])
        s0 = steps + 1
        load_xa = load_w(wx, wxv, 0, 256, s0)
        load_xd = load_w(wx, wxv, 768, 256, s0 + 1)
        load_xbc = load_w(wx, wxv, 256, 512, s0 + 2)
        load_z = load_w(wz, wzv, 0, 768, s0 + 3)
        load_xe = load_w(wx, wxv, 1024, 128, s0 + 4)
        load_n = load_w(wn, wnv, 0, 384, s0 + 5)
        load_frame(0).start()
        load_xa.start()
        load_h.start()
        load_xd.start()
        load_xbc.start()
        load_z.start()
        load_xe.start()
        load_n.start()
        for t in range(1, steps):
            load_frame(t).start()

        def zero_border(buf, i):
            edge = jnp.zeros((tile_w + 2, batch, ch), BF)
            buf[i, 0] = edge
            buf[i, tile_h + 1] = edge
            side = jnp.zeros((tile_h, 1, batch, ch), BF)
            buf[i, 1:tile_h + 1, 0:1] = side
            buf[i, 1:tile_h + 1, tile_w + 1:tile_w + 2] = side

        for i in range(2):
            zero_border(hb, i)
            zero_border(rb, i)

        @pl.loop(0, steps)
        def _(t):
            zero_border(xb, t)

        barrier = pltpu.get_barrier_semaphore()

        def greet(c, r):
            pl.semaphore_signal(barrier, inc=1, device_id={'cols': c, 'rows': r}, device_id_type=MESH)

        greet(col, other)

        @pl.when(has_left)
        def _():
            greet(left, row)
            greet(left, other)

        @pl.when(has_right)
        def _():
            greet(right, row)
            greet(right, other)

        pl.semaphore_wait(barrier, 1 + 2 * jnp.minimum(col, 1) + 2 * jnp.minimum(n_cols - 1 - col, 1))

        def copies(buf, i, slot):
            def rc(src, dst, k, c, r):
                return pltpu.make_async_remote_copy(
                    src_ref=buf.at[(i,) + src], dst_ref=buf.at[(i,) + dst], send_sem=send_sem.at[slot, k],
                    recv_sem=recv_sem.at[slot, k], device_id={'cols': c, 'rows': r}, device_id_type=MESH)
            rows = pl.ds(1, tile_h)
            return (
                rc((src_row, pl.ds(1, tile_w)), (dst_row, pl.ds(1, tile_w)), 0, col, other),
                rc((rows, 1), (rows, tile_w + 1), 1, left, row),
                rc((rows, tile_w), (rows, 0), 2, right, row),
                rc((src_row, 1), (dst_row, tile_w + 1), 3, left, other),
                rc((src_row, tile_w), (dst_row, 0), 4, right, other),
            )

        def send(buf, i, slot):
            cp = copies(buf, i, slot)
            cp[0].start()

            @pl.when(has_left)
            def _():
                cp[1].start()
                cp[3].start()

            @pl.when(has_right)
            def _():
                cp[2].start()
                cp[4].start()

        def wait_rows(buf, i, slot):
            copies(buf, i, slot)[0].wait_recv()

        def wait_cols(buf, i, slot):
            cp = copies(buf, i, slot)
            cp[0].wait_send()

            @pl.when(has_left)
            def _():
                cp[2].wait_recv()
                cp[4].wait_recv()
                cp[1].wait_send()
                cp[3].wait_send()

            @pl.when(has_right)
            def _():
                cp[1].wait_recv()
                cp[3].wait_recv()
                cp[2].wait_send()
                cp[4].wait_send()

        half_m = tile_h * half_w * batch

        def taps(buf, i, w, first, n, q, which):
            lhs, rhs = [], []
            for c in which[q]:
                for a in range(3):
                    lhs.append(buf[i, a:a + tile_h, q * half_w + c:q * half_w + c + half_w].reshape(half_m, ch))
                    rhs.append(w[(a * 3 + c) * ch:(a * 3 + c + 1) * ch, first:first + n])
            return lhs, rhs

        near6 = ((1, 2), (1, 0))
        far3 = ((0,), (2,))

        def product(lhs, rhs):
            return jnp.dot(jnp.concatenate(lhs, axis=1), jnp.concatenate(rhs, axis=0),
                           preferred_element_type=F32).reshape(tile_h, half_w, batch, -1)

        def six(buf, i, w, first, n=256):
            return [product(*taps(buf, i, w, first, n, q, near6)) for q in range(2)]

        def last(t, first_x, buf, i, w, first, n=256):
            out = []
            for q in range(2):
                lx, rx = taps(xb, t, wxv, first_x, n, q, far3)
                lh, rh = taps(buf, i, w, first, n, q, far3)
                out.append(product(lx + lh, rx + rh))
            return out

        def at(q):
            return (slice(None), slice(q * half_w, (q + 1) * half_w))

        def at_pad(q):
            return (slice(1, tile_h + 1), slice(1 + q * half_w, 1 + (q + 1) * half_w))

        def put(s, vals):
            for q in range(2):
                n = vals[q].shape[-1]
                gv[(s,) + at(q) + (slice(None), slice(0, n))] = vals[q]

        def add(s, vals):
            for q in range(2):
                n = vals[q].shape[-1]
                idx = (s,) + at(q) + (slice(None), slice(0, n))
                gv[idx] = gv[idx] + vals[q]

        def total(s, vals):
            return [vals[q] + gv[(s,) + at(q) + (slice(None), slice(0, vals[q].shape[-1]))] for q in range(2)]

        def lanes(g):
            return (slice(None), slice(g * L, (g + 1) * L))

        def b_of(first):
            return bias[0:1, first:first + L].reshape(1, 1, 1, L)

        def reset_part(v, g, q, par):
            r = sigmoid(v + b_of(ch + g * L))
            rb[(par,) + at_pad(q) + lanes(g)] = (r * hf[at(q) + lanes(g)]).astype(BF)

        def update_part(v, g, q):
            zf[at(q) + lanes(g)] = sigmoid(v + b_of(g * L))

        def state_part(v, g, q, nxt):
            idx = at(q) + lanes(g)
            n = jnp.tanh(v + b_of(2 * ch + g * L))
            z = zf[idx]
            h = (1.0 - z) * n + z * hf[idx]
            hf[idx] = h
            hb[(nxt,) + at_pad(q) + lanes(g)] = h.astype(BF)

        def store_step(t, nxt):
            return pltpu.make_async_copy(hb.at[(nxt,) + inner], h_seq.at[t], out_sem.at[nxt])

        h_slot, r_slot = steps, steps + 2

        load_frame(0).wait()
        send(xb, 0, 0)
        load_h.wait()

        @pl.loop(0, tile_h)
        def _(r):
            hb[0, 1 + r, 1:tile_w + 1] = hf[r].astype(BF)

        send(hb, 0, h_slot)
        load_xa.wait()
        wait_rows(xb, 0, 0)
        put(0, six(xb, 0, wxv, 0))

        @pl.loop(0, steps)
        def _(t):
            par = lax.rem(t, 2)
            nxt = 1 - par

            @pl.when(t == 0)
            def _():
                load_xd.wait()
                load_xbc.wait()

            put(3, six(xb, t, wxv, 768))
            put(1, six(xb, t, wxv, 256))
            put(2, six(xb, t, wxv, 512))
            wait_rows(hb, par, h_slot + par)

            @pl.when(t == 0)
            def _():
                load_z.wait()

            add(1, six(hb, par, wzv, 256))
            add(2, six(hb, par, wzv, 512))
            wait_cols(xb, t, t)
            wait_cols(hb, par, h_slot + par)

            @pl.when(t < steps - 1)
            def _():
                load_frame(t + 1).wait()
                send(xb, t + 1, t + 1)

            b_vals = total(1, last(t, 256, hb, par, wzv, 256))
            for q in range(2):
                update_part(b_vals[q][..., :L], 2, q)
                reset_part(b_vals[q][..., L:], 0, q, par)
            c_vals = total(2, last(t, 512, hb, par, wzv, 512))
            for q in range(2):
                reset_part(c_vals[q][..., :L], 1, q, par)
                reset_part(c_vals[q][..., L:], 2, q, par)
            add(0, six(hb, par, wzv, 0))
            send(rb, par, r_slot + par)

            @pl.when(t == 0)
            def _():
                load_xe.wait()
                load_n.wait()

            a_vals = total(0, last(t, 0, hb, par, wzv, 0))
            for q in range(2):
                update_part(a_vals[q][..., :L], 0, q)
                update_part(a_vals[q][..., L:], 1, q)
            put(4, six(xb, t, wxv, 1024, L))
            wait_rows(rb, par, r_slot + par)
            add(3, six(rb, par, wnv, 0))
            add(4, six(rb, par, wnv, 256, L))
            wait_cols(rb, par, r_slot + par)

            @pl.when(t > 0)
            def _():
                store_step(t - 1, par).wait()

            d_vals = total(3, last(t, 768, rb, par, wnv, 0))
            for q in range(2):
                state_part(d_vals[q][..., :L], 0, q, nxt)
                state_part(d_vals[q][..., L:], 1, q, nxt)
            add(4, last(t, 1024, rb, par, wnv, 256, L))

            def finish():
                for q in range(2):
                    state_part(gv[(4,) + at(q) + lanes(0)], 2, q, nxt)

            @pl.when(t < steps - 1)
            def _():
                wait_rows(xb, t + 1, t + 1)
                finish()
                put(0, six(xb, t + 1, wxv, 0))
                send(hb, nxt, h_slot + nxt)
                store_step(t, nxt).start()

            @pl.when(t == steps - 1)
            def _():
                finish()
                store_step(t, nxt).start()

        store_last = pltpu.make_async_copy(hf, h_last, load_sem.at[steps])
        store_last.start()
        store_step(steps - 1, steps % 2).wait()
        store_last.wait()

    return kernel


def solution(mesh):
    n_cols = mesh.shape['cols']
    frame_spec = P(None, 'batch', 'rows', 'cols', None)
    state_spec = P('batch', 'rows', 'cols', None)

    def local_fn(frames, h_init, w_x, w_hzr, w_hn, gate_bias):
        steps, batch, tile_h, tile_w, ch = frames.shape
        pad = (tile_h + 2, tile_w + 2, batch, ch)
        tile = (tile_h, tile_w, batch, ch)
        vmem = pltpu.VMEM
        any_spec = pl.BlockSpec(memory_space=pl.ANY)
        h_seq, h_last = pl.pallas_call(
            make_kernel(steps, tile_h, tile_w, batch, ch, n_cols),
            out_shape=(jax.ShapeDtypeStruct((steps,) + tile, BF), jax.ShapeDtypeStruct(tile, F32)),
            in_specs=[any_spec] * 5 + [pl.BlockSpec(memory_space=pltpu.VMEM)],
            out_specs=(any_spec, any_spec),
            scratch_shapes=[
                vmem((steps,) + pad, BF), vmem((2,) + pad, BF), vmem((2,) + pad, BF),
                vmem(tile, F32), vmem(tile, F32),
                vmem((5,) + tile[:3] + (256,), F32),
                vmem((9 * ch, 3 * ch), BF), vmem((9 * ch, 2 * ch), BF), vmem((9 * ch, ch), BF),
                pltpu.SemaphoreType.DMA((steps + 4, 5)), pltpu.SemaphoreType.DMA((steps + 4, 5)),
                pltpu.SemaphoreType.DMA((steps + 7,)), pltpu.SemaphoreType.DMA((2,)),
            ],
            compiler_params=pltpu.CompilerParams(collective_id=0, has_side_effects=True, vmem_limit_bytes=60 * 1024 * 1024),
            name='convgru',
        )(
            jnp.transpose(frames, (0, 2, 3, 1, 4)),
            jnp.transpose(h_init, (1, 2, 0, 3)),
            w_x.reshape(9 * ch, -1), w_hzr.reshape(9 * ch, -1), w_hn.reshape(9 * ch, -1), gate_bias.reshape(1, -1),
        )
        return jnp.transpose(h_seq, (0, 3, 1, 2, 4)), jnp.transpose(h_last, (2, 0, 1, 3))

    return jax.shard_map(local_fn, mesh=mesh, in_specs=(frame_spec, state_spec, P(), P(), P(), P()),
                         out_specs=(frame_spec, state_spec), check_vma=False)
```

time: 341 us -> 112 us (0.33)
  starting transfers between devices: 111 us -> 0 us
  Pallas kernels: 0 us -> 96.1 us
  matrix products: 90 us -> 0 us
  waiting for transfers between devices: 64.2 us -> 0 us
  local copies, waits for them, and re-layouts: 47 us -> 15.6 us
  other arithmetic: 24.6 us -> 0 us
    ppermute x36 -> x0, starting transfers between devices: 111 us -> none  [the longest x9 42.4 us: with_halo(): from_right = lax.ppermute(tall_tile[..., :width, :], 'cols', left_pairs)]
    pallas_call x0 -> x1, Pallas kernels: none -> 96.1 us  [local_fn(): pl.pallas_call(make_kernel(steps, tile_h, tile_w, batch, ch, n_cols), out...]
    dot_general x12 -> x0, matrix products: 90 us -> none  [im2col_conv(): jnp.einsum('...k,kg->...g', patches, w_mat, preferred_element_type=jnp.fl...]
    ppermute x36 -> x0, waiting for transfers between devices: 64.2 us -> none  [the longest x9 42.5 us: with_halo(): lax.ppermute(tall_tile[..., tile_w - width:, :], 'cols', right_pairs)]
    while x140 -> x0, local copies, waits for them, and re-layouts: 27 us -> none
    concatenate x17 -> x0, other arithmetic: 19.8 us -> none  [the longest x9 17.3 us: with_halo(): return jnp.concatenate([from_left, tall_tile, from_right], axis=-2)]
    unnamed x14 -> x8, local copies, waits for them, and re-layouts: 6.47 us -> 14.1 us
    dynamic_slice x8 -> x0, local copies, waits for them, and re-layouts: 7.23 us -> none  [local_fn(): h_last, h_seq = lax.scan(one_step, h_init, frames_pad)]
  transfers between devices with their start and end apart: 36 -> 0, of which waited for: 15 -> 0; matrix products, arithmetic and copies ran while one was open for 17% -> 0% of each run, Pallas kernels for 0% -> 0%
where the time goes in v1:
time: 112 us
  Pallas kernels  96.1 us (86%)
  local copies, waits for them, and re-layouts  15.6 us (14%)
    pallas_call x1, Pallas kernels, local_fn(): pl.pallas_call(make_kernel(steps, tile_h, tile_w, batch, ch, n_cols), out...  96.1 us
    unnamed x8, local copies, waits for them, and re-layouts  14.1 us

profile of v1, /device:TPU:97, one launch (start us, length us, event | category | flops | bytes accessed | tf_op | source)
XLA Modules:
  0.0 112.3 jit_solution(16339211747382002535)
XLA Ops:
  0.6 0.0 copy-start
  0.6 1.4 %reshape.19.bias = f32[1,1152]{1,0:T(1,128)} reshape(f32[1152]{0:T(1024)} %param.11) | data formatting | bytes 9216 | tf_op jit(solution)/shard_map/reshape | solution.py:348
  2.1 3.5 %copy.15 = f32[16,8,8,384]{3,0,2,1:T(8,128)} copy(f32[16,8,8,384]{3,2,1,0:T(8,128)} %param.7) | data formatting | bytes 3145728 | tf_op args[1]
  5.5 0.0 copy-done
  5.5 4.6 %copy.14 = bf16[4,16,8,8,384]{4,1,3,2,0:T(8,128)(2,1)} copy(bf16[4,16,8,8,384]{4,3,2,1,0:T(8,128)(2,1)S(1)} %copy-done) | data formatting | bytes 6291456 | tf_op args[0]
  10.2 96.1 %convgru.1 = (bf16[4,8,8,16,384]{4,3,2,1,0:T(8,128)(2,1)}, f32[8,8,16,384]{3,2,1,0:T(8,128)}) custom-call(bf16[4,8,8,16,384]{4,3,2,1,0:T(8,128)(2,1)} %bitcast.11, f32[8,8,16,384]{3,2,1,0:T(8,128)} %bitcast.13, bf16[3456,1152]{1,0:T(8,128)(2,1)} %bitcast.12, bf16[3456,768]{1,0:T(8,128)(2,1)} %bitcast.14, bf16[3456,384]{1,0:T(8,128)(2,1)} %bitcast.16, ...), custom_call_target="tpu_custom_call" | custom-call | tf_op jit(solution)/shard_map/convgru/pallas_call | solution.py:330
  106.2 0.0 copy-start.1
  106.3 4.4 %copy.10 = bf16[4,16,8,8,384]{4,3,2,1,0:T(8,128)(2,1)} copy(bf16[4,16,8,8,384]{4,1,3,2,0:T(8,128)(2,1)} %bitcast.15) | data formatting | bytes 6291456
  110.7 0.0 copy-done.1
  110.7 1.6 %copy.11 = f32[16,8,8,384]{3,2,1,0:T(8,128)} copy(f32[16,8,8,384]{3,0,2,1:T(8,128)S(1)} %bitcast.17) | data formatting | bytes 3145728
Async XLA Ops:
  0.6 4.9 %copy-start = (bf16[4,16,8,8,384]{4,3,2,1,0:T(8,128)(2,1)S(1)}, bf16[4,16,8,8,384]{4,3,2,1,0:T(8,128)(2,1)}, u32[]{:S(2)}) copy-start(bf16[4,16,8,8,384]{4,3,2,1,0:T(8,128)(2,1)} %param.6) | copy-start | bytes 9437188
  106.2 4.5 %copy-start.1 = (f32[8,8,16,384]{3,2,1,0:T(8,128)S(1)}, f32[8,8,16,384]{3,2,1,0:T(8,128)}, u32[]{:S(2)}) copy-start(f32[8,8,16,384]{3,2,1,0:T(8,128)} %get-tuple-element.5) | copy-start | bytes 4718596

commit v2 on v1

v2 whole, which is shorter than its diff:
```python
import jax
import jax.numpy as jnp
from jax import lax
from jax.experimental import pallas as pl
from jax.experimental.pallas import tpu as pltpu
from jax.sharding import PartitionSpec as P

MESH = pl.DeviceIdType.MESH
BF = jnp.bfloat16
F32 = jnp.float32
L = 128


def sigmoid(v):
    return 0.5 * jnp.tanh(0.5 * v) + 0.5


def make_kernel(steps, tile_h, tile_w, batch, ch, n_cols):
    half_w = tile_w // 2

    def kernel(frames, h0, wx, wz, wn, bias, h_seq, h_last,
               xs, hs, pm, xb, hb, rb, hf, zf, gv, wxv, wzv, wnv, send_sem, recv_sem, load_sem, out_sem):
        row = lax.axis_index('rows')
        col = lax.axis_index('cols')
        has_left = col > 0
        has_right = col < n_cols - 1
        left, right, other = col - 1, col + 1, 1 - row
        src_row = tile_h - (tile_h - 1) * row
        dst_row = (tile_h + 1) * row

        inner = (pl.ds(1, tile_h), pl.ds(1, tile_w))

        def load_frame(t):
            return pltpu.make_async_copy(frames.at[t], xs.at[t], load_sem.at[t])

        def load_w(src, dst, first, width, sem):
            return pltpu.make_async_copy(src.at[:, pl.ds(first, width)], dst.at[:, pl.ds(first, width)], load_sem.at[sem])

        s0 = steps + 1
        load_h = [pltpu.make_async_copy(h0.at[:, pl.ds(g * L, L)], hs.at[g], load_sem.at[s0 + 6 + g]) for g in range(ch // L)]
        load_xa = load_w(wx, wxv, 0, 256, s0)
        load_xd = load_w(wx, wxv, 768, 256, s0 + 1)
        load_xbc = load_w(wx, wxv, 256, 512, s0 + 2)
        load_z = load_w(wz, wzv, 0, 768, s0 + 3)
        load_xe = load_w(wx, wxv, 1024, 128, s0 + 4)
        load_n = load_w(wn, wnv, 0, 384, s0 + 5)
        load_frame(0).start()
        load_xa.start()
        for cp in load_h:
            cp.start()
        load_xd.start()
        load_xbc.start()
        load_z.start()
        load_xe.start()
        load_n.start()
        for t in range(1, steps):
            load_frame(t).start()

        def zero_border(buf, i):
            edge = jnp.zeros((tile_w + 2, batch, ch), BF)
            buf[i, 0] = edge
            buf[i, tile_h + 1] = edge
            side = jnp.zeros((tile_h, 1, batch, ch), BF)
            buf[i, 1:tile_h + 1, 0:1] = side
            buf[i, 1:tile_h + 1, tile_w + 1:tile_w + 2] = side

        for i in range(2):
            zero_border(hb, i)
            zero_border(rb, i)

        @pl.loop(0, steps)
        def _(t):
            zero_border(xb, t)

        barrier = pltpu.get_barrier_semaphore()

        def greet(c, r):
            pl.semaphore_signal(barrier, inc=1, device_id={'cols': c, 'rows': r}, device_id_type=MESH)

        greet(col, other)

        @pl.when(has_left)
        def _():
            greet(left, row)
            greet(left, other)

        @pl.when(has_right)
        def _():
            greet(right, row)
            greet(right, other)

        pl.semaphore_wait(barrier, 1 + 2 * jnp.minimum(col, 1) + 2 * jnp.minimum(n_cols - 1 - col, 1))

        def copies(buf, i, slot):
            def rc(src, dst, k, c, r):
                return pltpu.make_async_remote_copy(
                    src_ref=buf.at[(i,) + src], dst_ref=buf.at[(i,) + dst], send_sem=send_sem.at[slot, k],
                    recv_sem=recv_sem.at[slot, k], device_id={'cols': c, 'rows': r}, device_id_type=MESH)
            rows = pl.ds(1, tile_h)
            return (
                rc((src_row, pl.ds(1, tile_w)), (dst_row, pl.ds(1, tile_w)), 0, col, other),
                rc((rows, 1), (rows, tile_w + 1), 1, left, row),
                rc((rows, tile_w), (rows, 0), 2, right, row),
                rc((src_row, 1), (dst_row, tile_w + 1), 3, left, other),
                rc((src_row, tile_w), (dst_row, 0), 4, right, other),
            )

        def send(buf, i, slot):
            cp = copies(buf, i, slot)
            cp[0].start()

            @pl.when(has_left)
            def _():
                cp[1].start()
                cp[3].start()

            @pl.when(has_right)
            def _():
                cp[2].start()
                cp[4].start()

        def wait_rows(buf, i, slot):
            copies(buf, i, slot)[0].wait_recv()

        def wait_cols(buf, i, slot):
            cp = copies(buf, i, slot)
            cp[0].wait_send()

            @pl.when(has_left)
            def _():
                cp[2].wait_recv()
                cp[4].wait_recv()
                cp[1].wait_send()
                cp[3].wait_send()

            @pl.when(has_right)
            def _():
                cp[1].wait_recv()
                cp[3].wait_recv()
                cp[2].wait_send()
                cp[4].wait_send()

        def dot(lhs, rhs, rows, cols):
            return jnp.dot(jnp.concatenate(lhs, axis=1), jnp.concatenate(rhs, axis=0),
                           preferred_element_type=F32).reshape(rows, cols, batch, -1)

        def view(buf, i, a, rows, c, c0, c1):
            return buf[i, a:a + rows, c0 + c:c1 + c].reshape(rows * (c1 - c0) * batch, ch)

        def part(srcs, cs, c0, c1, n):
            if n > L:
                lhs, rhs = [], []
                for (buf, i, w, first) in srcs:
                    for c in cs:
                        for a in range(3):
                            lhs.append(view(buf, i, a, tile_h, c, c0, c1))
                            rhs.append(w[(a * 3 + c) * ch:(a * 3 + c + 1) * ch, first:first + n])
                return dot(lhs, rhs, tile_h, c1 - c0)
            lhs, rhs, lhs_2, rhs_2 = [], [], [], []
            for (buf, i, w, first) in srcs:
                for c in cs:
                    tap = [w[(a * 3 + c) * ch:(a * 3 + c + 1) * ch, first:first + n] for a in range(3)]
                    lhs.append(view(buf, i, 0, tile_h + 1, c, c0, c1))
                    rhs.append(jnp.concatenate(tap[:2], axis=1))
                    lhs_2.append(view(buf, i, 2, tile_h, c, c0, c1))
                    rhs_2.append(tap[2])
            pair = dot(lhs, rhs, tile_h + 1, c1 - c0)
            return pair[:tile_h, :, :, :L] + pair[1:, :, :, L:] + dot(lhs_2, rhs_2, tile_h, c1 - c0)

        halves = (((1, 2), 0, half_w), ((1, 0), half_w, tile_w))
        inner_far = (((0,), 1, half_w), ((2,), half_w, tile_w - 1))
        edge_far = (((0,), 0, 1), ((2,), tile_w - 1, tile_w))

        def slot_at(s, c0, c1, n):
            return (s, slice(None), slice(c0, c1), slice(None), slice(0, n))

        def put(s, srcs, n=256, which=halves):
            for (cs, c0, c1) in which:
                gv[slot_at(s, c0, c1, n)] = part(srcs, cs, c0, c1, n)

        def add(s, srcs, n=256, which=halves):
            for (cs, c0, c1) in which:
                idx = slot_at(s, c0, c1, n)
                gv[idx] = gv[idx] + part(srcs, cs, c0, c1, n)

        def finish(s, srcs, which, end, n=256):
            for (cs, c0, c1) in which:
                end(gv[slot_at(s, c0, c1, n)] + part(srcs, cs, c0, c1, n), c0, c1)

        def lanes(g):
            return (slice(None), slice(g * L, (g + 1) * L))

        def at(c0, c1):
            return (slice(None), slice(c0, c1))

        def at_pad(c0, c1):
            return (slice(1, tile_h + 1), slice(1 + c0, 1 + c1))

        def b_of(first):
            return bias[first:first + L].reshape(1, 1, 1, L)

        def reset_part(v, g, c0, c1, par):
            r = sigmoid(v + b_of(ch + g * L))
            rb[(par,) + at_pad(c0, c1) + lanes(g)] = (r * hf[at(c0, c1) + lanes(g)]).astype(BF)

        def update_part(v, g, c0, c1):
            zf[at(c0, c1) + lanes(g)] = sigmoid(v + b_of(g * L))

        def state_part(v, g, c0, c1, nxt):
            idx = at(c0, c1) + lanes(g)
            n = jnp.tanh(v + b_of(2 * ch + g * L))
            z = zf[idx]
            h = (1.0 - z) * n + z * hf[idx]
            hf[idx] = h
            hb[(nxt,) + at_pad(c0, c1) + lanes(g)] = h.astype(BF)

        def end_a(v, c0, c1):
            update_part(v[..., :L], 0, c0, c1)
            update_part(v[..., L:], 1, c0, c1)

        def end_b(par):
            def end(v, c0, c1):
                update_part(v[..., :L], 2, c0, c1)
                reset_part(v[..., L:], 0, c0, c1, par)
            return end

        def end_c(par):
            def end(v, c0, c1):
                reset_part(v[..., :L], 1, c0, c1, par)
                reset_part(v[..., L:], 2, c0, c1, par)
            return end

        def end_d(nxt):
            def end(v, c0, c1):
                state_part(v[..., :L], 0, c0, c1, nxt)
                state_part(v[..., L:], 1, c0, c1, nxt)
            return end

        def end_e(nxt):
            def end(v, c0, c1):
                state_part(v, 2, c0, c1, nxt)
            return end

        def permute_frame(t):
            for j in range(tile_h // 2):
                rows = [xs[t, b * tile_h * tile_w + j * 2 * tile_w:b * tile_h * tile_w + (j + 1) * 2 * tile_w] for b in range(batch)]
                out = jnp.dot(pm[...], jnp.concatenate(rows, axis=0), preferred_element_type=F32)
                xb[t, 1 + 2 * j:3 + 2 * j, 1:tile_w + 1] = out.astype(BF).reshape(2, tile_w, batch, ch)

        def make_permutation():
            n = 2 * tile_w * batch
            o = lax.broadcasted_iota(jnp.int32, (n, n), 0)
            i = lax.broadcasted_iota(jnp.int32, (n, n), 1)
            src = (o & 15) * 16 + (o >> 7) * 8 + ((o >> 4) & 7)
            pm[...] = jnp.where(i == src, 1.0, 0.0).astype(BF)

        def permute_state():
            @pl.loop(0, tile_h)
            def _(r):
                for c in range(tile_w):
                    for g in range(ch // L):
                        v = hs[g, pl.ds(r * tile_w + c, batch, stride=tile_h * tile_w), :]
                        hf[r, c, :, g * L:(g + 1) * L] = v
                        hb[0, 1 + r, 1 + c, :, g * L:(g + 1) * L] = v.astype(BF)

        def store_step(t, nxt):
            return pltpu.make_async_copy(hb.at[(nxt,) + inner], h_seq.at[t], out_sem.at[nxt])

        h_slot, r_slot = steps, steps + 2

        make_permutation()
        load_frame(0).wait()
        permute_frame(0)
        send(xb, 0, 0)
        for cp in load_h:
            cp.wait()
        permute_state()
        send(hb, 0, h_slot)
        load_xa.wait()
        wait_rows(xb, 0, 0)
        put(0, [(xb, 0, wxv, 0)], which=halves[:1])

        @pl.loop(0, steps)
        def _(t):
            par = lax.rem(t, 2)
            nxt = 1 - par

            @pl.when(t == 0)
            def _():
                load_xd.wait()
                load_xbc.wait()

            put(0, [(xb, t, wxv, 0)], which=halves[1:])
            put(3, [(xb, t, wxv, 768)])
            put(1, [(xb, t, wxv, 256)])
            put(2, [(xb, t, wxv, 512)])

            @pl.when(t < steps - 1)
            def _():
                load_frame(t + 1).wait()
                permute_frame(t + 1)

            wait_rows(hb, par, h_slot + par)

            @pl.when(t == 0)
            def _():
                load_z.wait()

            add(1, [(hb, par, wzv, 256)])
            add(2, [(hb, par, wzv, 512)])
            both_b = [(xb, t, wxv, 256), (hb, par, wzv, 256)]
            both_c = [(xb, t, wxv, 512), (hb, par, wzv, 512)]
            finish(1, both_b, inner_far, end_b(par))
            finish(2, both_c, inner_far, end_c(par))
            wait_cols(xb, t, t)
            wait_cols(hb, par, h_slot + par)

            @pl.when(t < steps - 1)
            def _():
                send(xb, t + 1, t + 1)

            both_a = [(xb, t, wxv, 0), (hb, par, wzv, 0)]
            finish(1, both_b, edge_far, end_b(par))
            finish(2, both_c, edge_far, end_c(par))
            add(0, both_a, which=edge_far)
            send(rb, par, r_slot + par)

            @pl.when(t == 0)
            def _():
                load_xe.wait()
                load_n.wait()

            add(0, [(hb, par, wzv, 0)])
            finish(0, both_a, inner_far, end_a)
            for (_, c0, c1) in edge_far:
                end_a(gv[slot_at(0, c0, c1, 256)], c0, c1)
            put(4, [(xb, t, wxv, 1024)], n=L)
            wait_rows(rb, par, r_slot + par)

            @pl.when(t > 0)
            def _():
                store_step(t - 1, par).wait()

            both_d = [(xb, t, wxv, 768), (rb, par, wnv, 0)]
            both_e = [(xb, t, wxv, 1024), (rb, par, wnv, 256)]
            add(3, [(rb, par, wnv, 0)])
            add(4, [(rb, par, wnv, 256)], n=L)
            finish(3, both_d, inner_far, end_d(nxt))
            finish(4, both_e, inner_far, end_e(nxt), n=L)
            wait_cols(rb, par, r_slot + par)

            @pl.when(t < steps - 1)
            def _():
                wait_rows(xb, t + 1, t + 1)

            finish(3, both_d, edge_far, end_d(nxt))
            finish(4, both_e, edge_far, end_e(nxt), n=L)

            @pl.when(t < steps - 1)
            def _():
                put(0, [(xb, t + 1, wxv, 0)], which=halves[:1])
                send(hb, nxt, h_slot + nxt)

            store_step(t, nxt).start()

        store_last = pltpu.make_async_copy(hf, h_last, load_sem.at[steps])
        store_last.start()
        store_step(steps - 1, steps % 2).wait()
        store_last.wait()

    return kernel


def solution(mesh):
    n_cols = mesh.shape['cols']
    frame_spec = P(None, 'batch', 'rows', 'cols', None)
    state_spec = P('batch', 'rows', 'cols', None)

    def local_fn(frames, h_init, w_x, w_hzr, w_hn, gate_bias):
        steps, batch, tile_h, tile_w, ch = frames.shape
        pad = (tile_h + 2, tile_w + 2, batch, ch)
        tile = (tile_h, tile_w, batch, ch)
        vmem = pltpu.VMEM
        any_spec = pl.BlockSpec(memory_space=pl.ANY)
        h_seq, h_last = pl.pallas_call(
            make_kernel(steps, tile_h, tile_w, batch, ch, n_cols),
            out_shape=(jax.ShapeDtypeStruct((steps,) + tile, BF), jax.ShapeDtypeStruct(tile, F32)),
            in_specs=[any_spec] * 5 + [pl.BlockSpec(memory_space=pltpu.VMEM)],
            out_specs=(any_spec, any_spec),
            scratch_shapes=[
                vmem((steps, tile_h * tile_w * batch, ch), BF), vmem((ch // L, tile_h * tile_w * batch, L), F32),
                vmem((2 * tile_w * batch, 2 * tile_w * batch), BF),
                vmem((steps,) + pad, BF), vmem((2,) + pad, BF), vmem((2,) + pad, BF),
                vmem(tile, F32), vmem(tile, F32),
                vmem((5,) + tile[:3] + (256,), F32),
                vmem((9 * ch, 3 * ch), BF), vmem((9 * ch, 2 * ch), BF), vmem((9 * ch, ch), BF),
                pltpu.SemaphoreType.DMA((steps + 4, 5)), pltpu.SemaphoreType.DMA((steps + 4, 5)),
                pltpu.SemaphoreType.DMA((steps + 10,)), pltpu.SemaphoreType.DMA((2,)),
            ],
            compiler_params=pltpu.CompilerParams(collective_id=0, has_side_effects=True, vmem_limit_bytes=60 * 1024 * 1024),
            name='convgru',
        )(
            frames.reshape(steps, -1, ch), h_init.reshape(-1, ch),
            w_x.reshape(9 * ch, -1), w_hzr.reshape(9 * ch, -1), w_hn.reshape(9 * ch, -1), gate_bias,
        )
        return jnp.transpose(h_seq, (0, 3, 1, 2, 4)), jnp.transpose(h_last, (2, 0, 1, 3))

    return jax.shard_map(local_fn, mesh=mesh, in_specs=(frame_spec, state_spec, P(), P(), P(), P()),
                         out_specs=(frame_spec, state_spec), check_vma=False)
```

time: 112 us -> 95.6 us (0.85)
  local copies, waits for them, and re-layouts: 15.6 us -> 6.07 us
  Pallas kernels: 96.1 us -> 88.8 us
    unnamed x8 -> x4, local copies, waits for them, and re-layouts: 14.1 us -> 6.07 us
    pallas_call x1, Pallas kernels: 96.1 us -> 88.8 us  [local_fn(): pl.pallas_call(make_kernel(steps, tile_h, tile_w, batch, ch, n_cols), out...]
    reshape x1 -> x0, local copies, waits for them, and re-layouts: 1.44 us -> none  [local_fn(): gate_bias.reshape(1, -1)]
where the time goes in v2:
time: 95.6 us; the launch traced here: 95.5 us
  Pallas kernels  88.8 us (93%)
  local copies, waits for them, and re-layouts  6.07 us (6%)
    pallas_call x1, Pallas kernels, local_fn(): pl.pallas_call(make_kernel(steps, tile_h, tile_w, batch, ch, n_cols), out...  88.8 us
    unnamed x4, local copies, waits for them, and re-layouts  6.07 us

profile of v2, /device:TPU:97, one launch (start us, length us, event | category | flops | bytes accessed | tf_op | source)
XLA Modules:
  0.0 95.5 jit_solution(17434405904510737139)
XLA Ops:
  0.6 88.8 %convgru.1 = (bf16[4,8,8,16,384]{4,3,2,1,0:T(8,128)(2,1)}, f32[8,8,16,384]{3,2,1,0:T(8,128)}) custom-call(bf16[4,1024,384]{2,1,0:T(8,128)(2,1)} %bitcast.9, f32[1024,384]{1,0:T(8,128)} %bitcast.12, bf16[3456,1152]{1,0:T(8,128)(2,1)} %bitcast.7, bf16[3456,768]{1,0:T(8,128)(2,1)} %bitcast.8, bf16[3456,384]{1,0:T(8,128)(2,1)} %bitcast.11, f32[1152]{0:T(1024)} %bias.1), custom_call_target="tpu_custom_call" | custom-call | tf_op jit(solution)/shard_map/convgru/pallas_call | solution.py:385
  89.4 0.0 copy-start
  89.4 4.4 %copy.8 = bf16[4,16,8,8,384]{4,3,2,1,0:T(8,128)(2,1)} copy(bf16[4,16,8,8,384]{4,1,3,2,0:T(8,128)(2,1)} %bitcast.10) | data formatting | bytes 6291456
  93.9 0.0 copy-done
  93.9 1.6 %copy.9 = f32[16,8,8,384]{3,2,1,0:T(8,128)} copy(f32[16,8,8,384]{3,0,2,1:T(8,128)S(1)} %bitcast.13) | data formatting | bytes 3145728
Async XLA Ops:
  89.4 4.5 %copy-start = (f32[8,8,16,384]{3,2,1,0:T(8,128)S(1)}, f32[8,8,16,384]{3,2,1,0:T(8,128)}, u32[]{:S(2)}) copy-start(f32[8,8,16,384]{3,2,1,0:T(8,128)} %get-tuple-element.5) | copy-start | bytes 4718596

commit v3 on v2

--- a/solution.py
+++ b/solution.py
@@ -22,9 +22,10 @@
                xs, hs, pm, xb, hb, rb, hf, zf, gv, wxv, wzv, wnv, send_sem, recv_sem, load_sem, out_sem):
         row = lax.axis_index('rows')
         col = lax.axis_index('cols')
-        has_left = col > 0
-        has_right = col < n_cols - 1
-        left, right, other = col - 1, col + 1, 1 - row
+        left, right, other = (col + n_cols - 1) % n_cols, (col + 1) % n_cols, 1 - row
+        spare = tile_w + 2
+        to_left = tile_w + 1 + (n_cols - col) // n_cols
+        to_right = spare * ((col + 1) // n_cols)
         src_row = tile_h - (tile_h - 1) * row
         dst_row = (tile_h + 1) * row
 
@@ -38,26 +39,24 @@
 
         s0 = steps + 1
         load_h = [pltpu.make_async_copy(h0.at[:, pl.ds(g * L, L)], hs.at[g], load_sem.at[s0 + 6 + g]) for g in range(ch // L)]
-        load_xa = load_w(wx, wxv, 0, 256, s0)
+        load_xabc = load_w(wx, wxv, 0, 768, s0)
         load_xd = load_w(wx, wxv, 768, 256, s0 + 1)
-        load_xbc = load_w(wx, wxv, 256, 512, s0 + 2)
         load_z = load_w(wz, wzv, 0, 768, s0 + 3)
         load_xe = load_w(wx, wxv, 1024, 128, s0 + 4)
         load_n = load_w(wn, wnv, 0, 384, s0 + 5)
         load_frame(0).start()
-        load_xa.start()
         for cp in load_h:
             cp.start()
+        load_xabc.start()
+        for t in range(1, steps):
+            load_frame(t).start()
+        load_z.start()
         load_xd.start()
-        load_xbc.start()
-        load_z.start()
         load_xe.start()
         load_n.start()
-        for t in range(1, steps):
-            load_frame(t).start()
 
         def zero_border(buf, i):
-            edge = jnp.zeros((tile_w + 2, batch, ch), BF)
+            edge = jnp.zeros((tile_w + 3, batch, ch), BF)
             buf[i, 0] = edge
             buf[i, tile_h + 1] = edge
             side = jnp.zeros((tile_h, 1, batch, ch), BF)
@@ -78,18 +77,10 @@
             pl.semaphore_signal(barrier, inc=1, device_id={'cols': c, 'rows': r}, device_id_type=MESH)
 
         greet(col, other)
-
-        @pl.when(has_left)
-        def _():
-            greet(left, row)
-            greet(left, other)
-
-        @pl.when(has_right)
-        def _():
-            greet(right, row)
-            greet(right, other)
-
-        pl.semaphore_wait(barrier, 1 + 2 * jnp.minimum(col, 1) + 2 * jnp.minimum(n_cols - 1 - col, 1))
+        for side_col in (left, right):
+            greet(side_col, row)
+            greet(side_col, other)
+        pl.semaphore_wait(barrier, 5)
 
         def copies(buf, i, slot):
             def rc(src, dst, k, c, r):
@@ -99,46 +90,25 @@
             rows = pl.ds(1, tile_h)
             return (
                 rc((src_row, pl.ds(1, tile_w)), (dst_row, pl.ds(1, tile_w)), 0, col, other),
-                rc((rows, 1), (rows, tile_w + 1), 1, left, row),
-                rc((rows, tile_w), (rows, 0), 2, right, row),
-                rc((src_row, 1), (dst_row, tile_w + 1), 3, left, other),
-                rc((src_row, tile_w), (dst_row, 0), 4, right, other),
+                rc((rows, 1), (rows, to_left), 1, left, row),
+                rc((rows, tile_w), (rows, to_right), 2, right, row),
+                rc((src_row, 1), (dst_row, to_left), 3, left, other),
+                rc((src_row, tile_w), (dst_row, to_right), 4, right, other),
             )
 
         def send(buf, i, slot):
-            cp = copies(buf, i, slot)
-            cp[0].start()
-
-            @pl.when(has_left)
-            def _():
-                cp[1].start()
-                cp[3].start()
-
-            @pl.when(has_right)
-            def _():
-                cp[2].start()
-                cp[4].start()
+            for cp in copies(buf, i, slot):
+                cp.start()
 
         def wait_rows(buf, i, slot):
             copies(buf, i, slot)[0].wait_recv()
 
         def wait_cols(buf, i, slot):
-            cp = copies(buf, i, slot)
-            cp[0].wait_send()
-
-            @pl.when(has_left)
-            def _():
-                cp[2].wait_recv()
-                cp[4].wait_recv()
-                cp[1].wait_send()
-                cp[3].wait_send()
-
-            @pl.when(has_right)
-            def _():
-                cp[1].wait_recv()
-                cp[3].wait_recv()
-                cp[2].wait_send()
-                cp[4].wait_send()
+            cps = copies(buf, i, slot)
+            for cp in cps[1:]:
+                cp.wait_recv()
+            for cp in cps:
+                cp.wait_send()
 
         def dot(lhs, rhs, rows, cols):
             return jnp.dot(jnp.concatenate(lhs, axis=1), jnp.concatenate(rhs, axis=0),
@@ -276,30 +246,21 @@
             cp.wait()
         permute_state()
         send(hb, 0, h_slot)
-        load_xa.wait()
+        store_step(0, 0).start()
+        for t in range(1, steps):
+            load_frame(t).wait()
+        for t in range(1, steps):
+            permute_frame(t)
+        load_xabc.wait()
         wait_rows(xb, 0, 0)
-        put(0, [(xb, 0, wxv, 0)], which=halves[:1])
 
         @pl.loop(0, steps)
         def _(t):
             par = lax.rem(t, 2)
             nxt = 1 - par
 
-            @pl.when(t == 0)
-            def _():
-                load_xd.wait()
-                load_xbc.wait()
-
-            put(0, [(xb, t, wxv, 0)], which=halves[1:])
-            put(3, [(xb, t, wxv, 768)])
             put(1, [(xb, t, wxv, 256)])
             put(2, [(xb, t, wxv, 512)])
-
-            @pl.when(t < steps - 1)
-            def _():
-                load_frame(t + 1).wait()
-                permute_frame(t + 1)
-
             wait_rows(hb, par, h_slot + par)
 
             @pl.when(t == 0)
@@ -312,21 +273,23 @@
             both_c = [(xb, t, wxv, 512), (hb, par, wzv, 512)]
             finish(1, both_b, inner_far, end_b(par))
             finish(2, both_c, inner_far, end_c(par))
+            put(0, [(xb, t, wxv, 0)])
             wait_cols(xb, t, t)
             wait_cols(hb, par, h_slot + par)
-
-            @pl.when(t < steps - 1)
-            def _():
-                send(xb, t + 1, t + 1)
-
+            store_step(jnp.maximum(t - 1, 0), par).wait()
             both_a = [(xb, t, wxv, 0), (hb, par, wzv, 0)]
             finish(1, both_b, edge_far, end_b(par))
             finish(2, both_c, edge_far, end_c(par))
             add(0, both_a, which=edge_far)
             send(rb, par, r_slot + par)
 
+            @pl.when(t < steps - 1)
+            def _():
+                send(xb, t + 1, t + 1)
+
             @pl.when(t == 0)
             def _():
+                load_xd.wait()
                 load_xe.wait()
                 load_n.wait()
 
@@ -334,13 +297,11 @@
             finish(0, both_a, inner_far, end_a)
             for (_, c0, c1) in edge_far:
                 end_a(gv[slot_at(0, c0, c1, 256)], c0, c1)
+            put(3, [(xb, t, wxv, 768)])
+            wait_rows(rb, par, r_slot + par)
+
+
             put(4, [(xb, t, wxv, 1024)], n=L)
-            wait_rows(rb, par, r_slot + par)
-
-            @pl.when(t > 0)
-            def _():
-                store_step(t - 1, par).wait()
-
             both_d = [(xb, t, wxv, 768), (rb, par, wnv, 0)]
             both_e = [(xb, t, wxv, 1024), (rb, par, wnv, 256)]
             add(3, [(rb, par, wnv, 0)])
@@ -348,18 +309,13 @@
             finish(3, both_d, inner_far, end_d(nxt))
             finish(4, both_e, inner_far, end_e(nxt), n=L)
             wait_cols(rb, par, r_slot + par)
+            finish(3, both_d, edge_far, end_d(nxt))
+            finish(4, both_e, edge_far, end_e(nxt), n=L)
 
             @pl.when(t < steps - 1)
             def _():
+                send(hb, nxt, h_slot + nxt)
                 wait_rows(xb, t + 1, t + 1)
-
-            finish(3, both_d, edge_far, end_d(nxt))
-            finish(4, both_e, edge_far, end_e(nxt), n=L)
-
-            @pl.when(t < steps - 1)
-            def _():
-                put(0, [(xb, t + 1, wxv, 0)], which=halves[:1])
-                send(hb, nxt, h_slot + nxt)
 
             store_step(t, nxt).start()
 
@@ -378,7 +334,7 @@
 
     def local_fn(frames, h_init, w_x, w_hzr, w_hn, gate_bias):
         steps, batch, tile_h, tile_w, ch = frames.shape
-        pad = (tile_h + 2, tile_w + 2, batch, ch)
+        pad = (tile_h + 2, tile_w + 3, batch, ch)
         tile = (tile_h, tile_w, batch, ch)
         vmem = pltpu.VMEM
         any_spec = pl.BlockSpec(memory_space=pl.ANY)

time: 95.6 us -> 95.3 us (level)
  the two profiles are of different devices: /device:TPU:97 before, /device:TPU:1 now
where the time goes in v3:
time: 95.3 us; the launch traced here: 95.2 us
  Pallas kernels  88.5 us (93%)
  local copies, waits for them, and re-layouts  6.07 us (6%)
    pallas_call x1, Pallas kernels, local_fn(): pl.pallas_call(make_kernel(steps, tile_h, tile_w, batch, ch, n_cols), out...  88.5 us
    unnamed x4, local copies, waits for them, and re-layouts  6.07 us

profile of v3, /device:TPU:1, one launch (start us, length us, event | category | flops | bytes accessed | tf_op | source)
XLA Modules:
  0.0 95.2 jit_solution(6987224520258747899)
XLA Ops:
  0.6 88.5 %convgru.1 = (bf16[4,8,8,16,384]{4,3,2,1,0:T(8,128)(2,1)}, f32[8,8,16,384]{3,2,1,0:T(8,128)}) custom-call(bf16[4,1024,384]{2,1,0:T(8,128)(2,1)} %bitcast.9, f32[1024,384]{1,0:T(8,128)} %bitcast.12, bf16[3456,1152]{1,0:T(8,128)(2,1)} %bitcast.7, bf16[3456,768]{1,0:T(8,128)(2,1)} %bitcast.8, bf16[3456,384]{1,0:T(8,128)(2,1)} %bitcast.11, f32[1152]{0:T(1024)} %bias.1), custom_call_target="tpu_custom_call" | custom-call | tf_op jit(solution)/shard_map/convgru/pallas_call | solution.py:341
  89.1 0.0 copy-start
  89.1 4.4 %copy.8 = bf16[4,16,8,8,384]{4,3,2,1,0:T(8,128)(2,1)} copy(bf16[4,16,8,8,384]{4,1,3,2,0:T(8,128)(2,1)} %bitcast.10) | data formatting | bytes 6291456
  93.6 0.0 copy-done
  93.6 1.6 %copy.9 = f32[16,8,8,384]{3,2,1,0:T(8,128)} copy(f32[16,8,8,384]{3,0,2,1:T(8,128)S(1)} %bitcast.13) | data formatting | bytes 3145728
Async XLA Ops:
  89.1 4.5 %copy-start = (f32[8,8,16,384]{3,2,1,0:T(8,128)S(1)}, f32[8,8,16,384]{3,2,1,0:T(8,128)}, u32[]{:S(2)}) copy-start(f32[8,8,16,384]{3,2,1,0:T(8,128)} %get-tuple-element.5) | copy-start | bytes 4718596

commit v4 on v3

--- a/solution.py
+++ b/solution.py
@@ -22,10 +22,12 @@
                xs, hs, pm, xb, hb, rb, hf, zf, gv, wxv, wzv, wnv, send_sem, recv_sem, load_sem, out_sem):
         row = lax.axis_index('rows')
         col = lax.axis_index('cols')
-        left, right, other = (col + n_cols - 1) % n_cols, (col + 1) % n_cols, 1 - row
-        spare = tile_w + 2
-        to_left = tile_w + 1 + (n_cols - col) // n_cols
-        to_right = spare * ((col + 1) // n_cols)
+        other = 1 - row
+        first = (n_cols - col) // n_cols
+        final = (col + 1) // n_cols
+        left, right = col - 1 + first, col + 1 - final
+        left_row, right_row = row + first * (1 - 2 * row), row + final * (1 - 2 * row)
+        to_left, to_right = tile_w + 1 + first, final * (tile_w + 2)
         src_row = tile_h - (tile_h - 1) * row
         dst_row = (tile_h + 1) * row
 
@@ -38,8 +40,10 @@
             return pltpu.make_async_copy(src.at[:, pl.ds(first, width)], dst.at[:, pl.ds(first, width)], load_sem.at[sem])
 
         s0 = steps + 1
-        load_h = [pltpu.make_async_copy(h0.at[:, pl.ds(g * L, L)], hs.at[g], load_sem.at[s0 + 6 + g]) for g in range(ch // L)]
-        load_xabc = load_w(wx, wxv, 0, 768, s0)
+        load_h = [pltpu.make_async_copy(h0.at[:, :, pl.ds(g * L, L)], hs.at[g, :, pl.ds(0, tile_h * tile_w)], load_sem.at[s0 + 6 + g])
+                  for g in range(ch // L)]
+        load_xbc = load_w(wx, wxv, 256, 512, s0)
+        load_xa = load_w(wx, wxv, 0, 256, s0 + 2)
         load_xd = load_w(wx, wxv, 768, 256, s0 + 1)
         load_z = load_w(wz, wzv, 0, 768, s0 + 3)
         load_xe = load_w(wx, wxv, 1024, 128, s0 + 4)
@@ -47,9 +51,10 @@
         load_frame(0).start()
         for cp in load_h:
             cp.start()
-        load_xabc.start()
+        load_xbc.start()
         for t in range(1, steps):
             load_frame(t).start()
+        load_xa.start()
         load_z.start()
         load_xd.start()
         load_xe.start()
@@ -77,23 +82,24 @@
             pl.semaphore_signal(barrier, inc=1, device_id={'cols': c, 'rows': r}, device_id_type=MESH)
 
         greet(col, other)
-        for side_col in (left, right):
-            greet(side_col, row)
-            greet(side_col, other)
+        greet(left, left_row)
+        greet(left, other)
+        greet(right, right_row)
+        greet(right, other)
         pl.semaphore_wait(barrier, 5)
 
-        def copies(buf, i, slot):
-            def rc(src, dst, k, c, r):
+        def copies(buf, i, slot, first=first, final=final):
+            def rc(src, dst, k, land, c, r):
                 return pltpu.make_async_remote_copy(
                     src_ref=buf.at[(i,) + src], dst_ref=buf.at[(i,) + dst], send_sem=send_sem.at[slot, k],
-                    recv_sem=recv_sem.at[slot, k], device_id={'cols': c, 'rows': r}, device_id_type=MESH)
+                    recv_sem=recv_sem.at[slot, land], device_id={'cols': c, 'rows': r}, device_id_type=MESH)
             rows = pl.ds(1, tile_h)
             return (
-                rc((src_row, pl.ds(1, tile_w)), (dst_row, pl.ds(1, tile_w)), 0, col, other),
-                rc((rows, 1), (rows, to_left), 1, left, row),
-                rc((rows, tile_w), (rows, to_right), 2, right, row),
-                rc((src_row, 1), (dst_row, to_left), 3, left, other),
-                rc((src_row, tile_w), (dst_row, to_right), 4, right, other),
+                rc((src_row, pl.ds(1, tile_w)), (dst_row, pl.ds(1, tile_w)), 0, 0, col, other),
+                rc((rows, 1), (rows, to_left), 1, 1 + first, left, left_row),
+                rc((rows, tile_w), (rows, to_right), 2, 2 - final, right, right_row),
+                rc((src_row, 1), (dst_row, to_left), 3, 3 + first, left, other),
+                rc((src_row, tile_w), (dst_row, to_right), 4, 4 - final, right, other),
             )
 
         def send(buf, i, slot):
@@ -104,10 +110,9 @@
             copies(buf, i, slot)[0].wait_recv()
 
         def wait_cols(buf, i, slot):
-            cps = copies(buf, i, slot)
-            for cp in cps[1:]:
+            for cp in copies(buf, i, slot, 0, 0)[1:]:
                 cp.wait_recv()
-            for cp in cps:
+            for cp in copies(buf, i, slot):
                 cp.wait_send()
 
         def dot(lhs, rhs, rows, cols):
@@ -127,15 +132,19 @@
                             rhs.append(w[(a * 3 + c) * ch:(a * 3 + c + 1) * ch, first:first + n])
                 return dot(lhs, rhs, tile_h, c1 - c0)
             lhs, rhs, lhs_2, rhs_2 = [], [], [], []
-            for (buf, i, w, first) in srcs:
+            both = len(cs) == 2
+            low = min(cs)
+            for (buf, i, w, first_n) in srcs:
+                tap = {(a, c): w[(a * 3 + c) * ch:(a * 3 + c + 1) * ch, first_n:first_n + n] for c in cs for a in range(3)}
                 for c in cs:
-                    tap = [w[(a * 3 + c) * ch:(a * 3 + c + 1) * ch, first:first + n] for a in range(3)]
                     lhs.append(view(buf, i, 0, tile_h + 1, c, c0, c1))
-                    rhs.append(jnp.concatenate(tap[:2], axis=1))
-                    lhs_2.append(view(buf, i, 2, tile_h, c, c0, c1))
-                    rhs_2.append(tap[2])
+                    rhs.append(jnp.concatenate([tap[0, c], tap[1, c]], axis=1))
+                lhs_2.append(view(buf, i, 2, tile_h, low, c0, c1 + both))
+                rhs_2.append(jnp.concatenate([tap[2, low], tap[2, low + 1]], axis=1) if both else tap[2, low])
             pair = dot(lhs, rhs, tile_h + 1, c1 - c0)
-            return pair[:tile_h, :, :, :L] + pair[1:, :, :, L:] + dot(lhs_2, rhs_2, tile_h, c1 - c0)
+            out = pair[:tile_h, :, :, :L] + pair[1:, :, :, L:]
+            pair = dot(lhs_2, rhs_2, tile_h, c1 - c0 + both)
+            return out + (pair[:, :-1, :, :L] + pair[:, 1:, :, L:] if both else pair)
 
         halves = (((1, 2), 0, half_w), ((1, 0), half_w, tile_w))
         inner_far = (((0,), 1, half_w), ((2,), half_w, tile_w - 1))
@@ -224,12 +233,14 @@
             src = (o & 15) * 16 + (o >> 7) * 8 + ((o >> 4) & 7)
             pm[...] = jnp.where(i == src, 1.0, 0.0).astype(BF)
 
+        pitch = tile_h * tile_w + 8
+
         def permute_state():
             @pl.loop(0, tile_h)
             def _(r):
                 for c in range(tile_w):
                     for g in range(ch // L):
-                        v = hs[g, pl.ds(r * tile_w + c, batch, stride=tile_h * tile_w), :]
+                        v = hs.at[g].reshape(batch * pitch, L)[pl.ds(r * tile_w + c, batch, stride=pitch), :]
                         hf[r, c, :, g * L:(g + 1) * L] = v
                         hb[0, 1 + r, 1 + c, :, g * L:(g + 1) * L] = v.astype(BF)
 
@@ -251,7 +262,7 @@
             load_frame(t).wait()
         for t in range(1, steps):
             permute_frame(t)
-        load_xabc.wait()
+        load_xbc.wait()
         wait_rows(xb, 0, 0)
 
         @pl.loop(0, steps)
@@ -265,6 +276,7 @@
 
             @pl.when(t == 0)
             def _():
+                load_xa.wait()
                 load_z.wait()
 
             add(1, [(hb, par, wzv, 256)])
@@ -301,11 +313,10 @@
             wait_rows(rb, par, r_slot + par)
 
 
-            put(4, [(xb, t, wxv, 1024)], n=L)
             both_d = [(xb, t, wxv, 768), (rb, par, wnv, 0)]
             both_e = [(xb, t, wxv, 1024), (rb, par, wnv, 256)]
             add(3, [(rb, par, wnv, 0)])
-            add(4, [(rb, par, wnv, 256)], n=L)
+            put(4, both_e, n=L)
             finish(3, both_d, inner_far, end_d(nxt))
             finish(4, both_e, inner_far, end_e(nxt), n=L)
             wait_cols(rb, par, r_slot + par)
@@ -344,7 +355,7 @@
             in_specs=[any_spec] * 5 + [pl.BlockSpec(memory_space=pltpu.VMEM)],
             out_specs=(any_spec, any_spec),
             scratch_shapes=[
-                vmem((steps, tile_h * tile_w * batch, ch), BF), vmem((ch // L, tile_h * tile_w * batch, L), F32),
+                vmem((steps, tile_h * tile_w * batch, ch), BF), vmem((ch // L, batch, tile_h * tile_w + 8, L), F32),
                 vmem((2 * tile_w * batch, 2 * tile_w * batch), BF),
                 vmem((steps,) + pad, BF), vmem((2,) + pad, BF), vmem((2,) + pad, BF),
                 vmem(tile, F32), vmem(tile, F32),
@@ -356,7 +367,7 @@
             compiler_params=pltpu.CompilerParams(collective_id=0, has_side_effects=True, vmem_limit_bytes=60 * 1024 * 1024),
             name='convgru',
         )(
-            frames.reshape(steps, -1, ch), h_init.reshape(-1, ch),
+            frames.reshape(steps, -1, ch), h_init.reshape(batch, -1, ch),
             w_x.reshape(9 * ch, -1), w_hzr.reshape(9 * ch, -1), w_hn.reshape(9 * ch, -1), gate_bias,
         )
         return jnp.transpose(h_seq, (0, 3, 1, 2, 4)), jnp.transpose(h_last, (2, 0, 1, 3))

time: 95.3 us -> 88.4 us (0.928)
  the two profiles are of different devices: /device:TPU:1 before, /device:TPU:97 now
where the time goes in v4:
time: 88.4 us; the launch traced here: 88.2 us
  Pallas kernels  81.5 us (92%)
  local copies, waits for them, and re-layouts  6.07 us (7%)
    pallas_call x1, Pallas kernels, local_fn(): pl.pallas_call(make_kernel(steps, tile_h, tile_w, batch, ch, n_cols), out...  81.5 us
    unnamed x4, local copies, waits for them, and re-layouts  6.07 us

profile of v4, /device:TPU:97, one launch (start us, length us, event | category | flops | bytes accessed | tf_op | source)
XLA Modules:
  0.0 88.2 jit_solution(17929096560075572281)
XLA Ops:
  0.6 81.5 %convgru.1 = (bf16[4,8,8,16,384]{4,3,2,1,0:T(8,128)(2,1)}, f32[8,8,16,384]{3,2,1,0:T(8,128)}) custom-call(bf16[4,1024,384]{2,1,0:T(8,128)(2,1)} %bitcast.9, f32[16,64,384]{2,1,0:T(8,128)} %bitcast.12, bf16[3456,1152]{1,0:T(8,128)(2,1)} %bitcast.7, bf16[3456,768]{1,0:T(8,128)(2,1)} %bitcast.8, bf16[3456,384]{1,0:T(8,128)(2,1)} %bitcast.11, f32[1152]{0:T(1024)} %bias.1), custom_call_target="tpu_custom_call" | custom-call | tf_op jit(solution)/shard_map/convgru/pallas_call | solution.py:352
  82.1 0.0 copy-start
  82.2 4.4 %copy.8 = bf16[4,16,8,8,384]{4,3,2,1,0:T(8,128)(2,1)} copy(bf16[4,16,8,8,384]{4,1,3,2,0:T(8,128)(2,1)} %bitcast.10) | data formatting | bytes 6291456
  86.6 0.0 copy-done
  86.6 1.6 %copy.9 = f32[16,8,8,384]{3,2,1,0:T(8,128)} copy(f32[16,8,8,384]{3,0,2,1:T(8,128)S(1)} %bitcast.13) | data formatting | bytes 3145728
Async XLA Ops:
  82.1 4.5 %copy-start = (f32[8,8,16,384]{3,2,1,0:T(8,128)S(1)}, f32[8,8,16,384]{3,2,1,0:T(8,128)}, u32[]{:S(2)}) copy-start(f32[8,8,16,384]{3,2,1,0:T(8,128)} %get-tuple-element.5) | copy-start | bytes 4718596

commit v5 on v4

--- a/solution.py
+++ b/solution.py
@@ -19,7 +19,7 @@
     half_w = tile_w // 2
 
     def kernel(frames, h0, wx, wz, wn, bias, h_seq, h_last,
-               xs, hs, pm, xb, hb, rb, hf, zf, gv, wxv, wzv, wnv, send_sem, recv_sem, load_sem, out_sem):
+               xs, hs, ob, pm, xb, hb, rb, hf, zf, gv, wxv, wzv, wnv, send_sem, recv_sem, load_sem, out_sem):
         row = lax.axis_index('rows')
         col = lax.axis_index('cols')
         other = 1 - row
@@ -30,6 +30,17 @@
         to_left, to_right = tile_w + 1 + first, final * (tile_w + 2)
         src_row = tile_h - (tile_h - 1) * row
         dst_row = (tile_h + 1) * row
+
+        barrier = pltpu.get_barrier_semaphore()
+
+        def greet(c, r):
+            pl.semaphore_signal(barrier, inc=1, device_id={'cols': c, 'rows': r}, device_id_type=MESH)
+
+        greet(col, other)
+        greet(left, left_row)
+        greet(left, other)
+        greet(right, right_row)
+        greet(right, other)
 
         inner = (pl.ds(1, tile_h), pl.ds(1, tile_w))
 
@@ -61,32 +72,25 @@
         load_n.start()
 
         def zero_border(buf, i):
-            edge = jnp.zeros((tile_w + 3, batch, ch), BF)
-            buf[i, 0] = edge
-            buf[i, tile_h + 1] = edge
-            side = jnp.zeros((tile_h, 1, batch, ch), BF)
-            buf[i, 1:tile_h + 1, 0:1] = side
-            buf[i, 1:tile_h + 1, tile_w + 1:tile_w + 2] = side
-
-        for i in range(2):
-            zero_border(hb, i)
-            zero_border(rb, i)
-
-        @pl.loop(0, steps)
-        def _(t):
-            zero_border(xb, t)
-
-        barrier = pltpu.get_barrier_semaphore()
-
-        def greet(c, r):
-            pl.semaphore_signal(barrier, inc=1, device_id={'cols': c, 'rows': r}, device_id_type=MESH)
-
-        greet(col, other)
-        greet(left, left_row)
-        greet(left, other)
-        greet(right, right_row)
-        greet(right, other)
-        pl.semaphore_wait(barrier, 5)
+            buf[i, (tile_h + 1) * row] = jnp.zeros((tile_w + 3, batch, ch), BF)
+
+            @pl.when(first == 1)
+            def _():
+                buf[i, :, 0:1] = jnp.zeros((tile_h + 2, 1, batch, ch), BF)
+
+            @pl.when(final == 1)
+            def _():
+                buf[i, :, tile_w + 1:tile_w + 2] = jnp.zeros((tile_h + 2, 1, batch, ch), BF)
+
+        def zero_borders():
+            @pl.loop(0, 2)
+            def _(i):
+                zero_border(hb, i)
+                zero_border(rb, i)
+
+            @pl.loop(0, steps)
+            def _(t):
+                zero_border(xb, t)
 
         def copies(buf, i, slot, first=first, final=final):
             def rc(src, dst, k, land, c, r):
@@ -166,6 +170,11 @@
             for (cs, c0, c1) in which:
                 end(gv[slot_at(s, c0, c1, n)] + part(srcs, cs, c0, c1, n), c0, c1)
 
+        pitch = tile_h * tile_w + 8
+
+        def flat(g):
+            return hs.at[g].reshape(batch * pitch, L)
+
         def lanes(g):
             return (slice(None), slice(g * L, (g + 1) * L))
 
@@ -192,6 +201,9 @@
             h = (1.0 - z) * n + z * hf[idx]
             hf[idx] = h
             hb[(nxt,) + at_pad(c0, c1) + lanes(g)] = h.astype(BF)
+            for r in range(tile_h):
+                for c in range(c0, c1):
+                    flat(g)[pl.ds(r * tile_w + c, batch, stride=pitch), :] = h[r, c - c0]
 
         def end_a(v, c0, c1):
             update_part(v[..., :L], 0, c0, c1)
@@ -233,31 +245,35 @@
             src = (o & 15) * 16 + (o >> 7) * 8 + ((o >> 4) & 7)
             pm[...] = jnp.where(i == src, 1.0, 0.0).astype(BF)
 
-        pitch = tile_h * tile_w + 8
-
         def permute_state():
             @pl.loop(0, tile_h)
             def _(r):
                 for c in range(tile_w):
                     for g in range(ch // L):
-                        v = hs.at[g].reshape(batch * pitch, L)[pl.ds(r * tile_w + c, batch, stride=pitch), :]
+                        v = flat(g)[pl.ds(r * tile_w + c, batch, stride=pitch), :]
                         hf[r, c, :, g * L:(g + 1) * L] = v
                         hb[0, 1 + r, 1 + c, :, g * L:(g + 1) * L] = v.astype(BF)
 
-        def store_step(t, nxt):
-            return pltpu.make_async_copy(hb.at[(nxt,) + inner], h_seq.at[t], out_sem.at[nxt])
+        def round_state():
+            for b in range(batch):
+                for g in range(ch // L):
+                    ob[b * tile_h * tile_w:(b + 1) * tile_h * tile_w, g * L:(g + 1) * L] = hs[g, b, 0:tile_h * tile_w].astype(BF)
+
+        def store_step(t):
+            return pltpu.make_async_copy(ob, h_seq.at[t], out_sem.at[0])
 
         h_slot, r_slot = steps, steps + 2
 
         make_permutation()
+        zero_borders()
         load_frame(0).wait()
         permute_frame(0)
+        pl.semaphore_wait(barrier, 5)
         send(xb, 0, 0)
         for cp in load_h:
             cp.wait()
         permute_state()
         send(hb, 0, h_slot)
-        store_step(0, 0).start()
         for t in range(1, steps):
             load_frame(t).wait()
         for t in range(1, steps):
@@ -286,9 +302,11 @@
             finish(1, both_b, inner_far, end_b(par))
             finish(2, both_c, inner_far, end_c(par))
             put(0, [(xb, t, wxv, 0)])
+            round_state()
             wait_cols(xb, t, t)
             wait_cols(hb, par, h_slot + par)
-            store_step(jnp.maximum(t - 1, 0), par).wait()
+            store = store_step(jnp.maximum(t - 1, 0))
+            store.start()
             both_a = [(xb, t, wxv, 0), (hb, par, wzv, 0)]
             finish(1, both_b, edge_far, end_b(par))
             finish(2, both_c, edge_far, end_c(par))
@@ -320,6 +338,7 @@
             finish(3, both_d, inner_far, end_d(nxt))
             finish(4, both_e, inner_far, end_e(nxt), n=L)
             wait_cols(rb, par, r_slot + par)
+            store.wait()
             finish(3, both_d, edge_far, end_d(nxt))
             finish(4, both_e, edge_far, end_e(nxt), n=L)
 
@@ -328,12 +347,16 @@
                 send(hb, nxt, h_slot + nxt)
                 wait_rows(xb, t + 1, t + 1)
 
-            store_step(t, nxt).start()
-
-        store_last = pltpu.make_async_copy(hf, h_last, load_sem.at[steps])
-        store_last.start()
-        store_step(steps - 1, steps % 2).wait()
-        store_last.wait()
+        store_last = [pltpu.make_async_copy(hs.at[g, :, pl.ds(0, tile_h * tile_w)], h_last.at[:, :, pl.ds(g * L, L)],
+                                            load_sem.at[s0 + 6 + g]) for g in range(ch // L)]
+        for cp in store_last:
+            cp.start()
+        round_state()
+        store = store_step(steps - 1)
+        store.start()
+        for cp in store_last:
+            cp.wait()
+        store.wait()
 
     return kernel
 
@@ -351,18 +374,19 @@
         any_spec = pl.BlockSpec(memory_space=pl.ANY)
         h_seq, h_last = pl.pallas_call(
             make_kernel(steps, tile_h, tile_w, batch, ch, n_cols),
-            out_shape=(jax.ShapeDtypeStruct((steps,) + tile, BF), jax.ShapeDtypeStruct(tile, F32)),
+            out_shape=(jax.ShapeDtypeStruct((steps, tile_h * tile_w * batch, ch), BF),
+                       jax.ShapeDtypeStruct((batch, tile_h * tile_w, ch), F32)),
             in_specs=[any_spec] * 5 + [pl.BlockSpec(memory_space=pltpu.VMEM)],
             out_specs=(any_spec, any_spec),
             scratch_shapes=[
                 vmem((steps, tile_h * tile_w * batch, ch), BF), vmem((ch // L, batch, tile_h * tile_w + 8, L), F32),
-                vmem((2 * tile_w * batch, 2 * tile_w * batch), BF),
+                vmem((tile_h * tile_w * batch, ch), BF), vmem((2 * tile_w * batch, 2 * tile_w * batch), BF),
                 vmem((steps,) + pad, BF), vmem((2,) + pad, BF), vmem((2,) + pad, BF),
                 vmem(tile, F32), vmem(tile, F32),
                 vmem((5,) + tile[:3] + (256,), F32),
                 vmem((9 * ch, 3 * ch), BF), vmem((9 * ch, 2 * ch), BF), vmem((9 * ch, ch), BF),
                 pltpu.SemaphoreType.DMA((steps + 4, 5)), pltpu.SemaphoreType.DMA((steps + 4, 5)),
-                pltpu.SemaphoreType.DMA((steps + 10,)), pltpu.SemaphoreType.DMA((2,)),
+                pltpu.SemaphoreType.DMA((steps + 10,)), pltpu.SemaphoreType.DMA((1,)),
             ],
             compiler_params=pltpu.CompilerParams(collective_id=0, has_side_effects=True, vmem_limit_bytes=60 * 1024 * 1024),
             name='convgru',
@@ -370,7 +394,7 @@
             frames.reshape(steps, -1, ch), h_init.reshape(batch, -1, ch),
             w_x.reshape(9 * ch, -1), w_hzr.reshape(9 * ch, -1), w_hn.reshape(9 * ch, -1), gate_bias,
         )
-        return jnp.transpose(h_seq, (0, 3, 1, 2, 4)), jnp.transpose(h_last, (2, 0, 1, 3))
+        return h_seq.reshape(frames.shape), h_last.reshape(h_init.shape)
 
     return jax.shard_map(local_fn, mesh=mesh, in_specs=(frame_spec, state_spec, P(), P(), P(), P()),
                          out_specs=(frame_spec, state_spec), check_vma=False)

time: 88.4 us -> 87.5 us (0.990)
  local copies, waits for them, and re-layouts: 6.07 us -> 5.16 us
    unnamed x4, local copies, waits for them, and re-layouts: 6.07 us -> 5.16 us
where the time goes in v5:
time: 87.5 us; the launch traced here: 87.3 us
  Pallas kernels  81.5 us (93%)
  local copies, waits for them, and re-layouts  5.16 us (6%)
    pallas_call x1, Pallas kernels, local_fn(): pl.pallas_call(make_kernel(steps, tile_h, tile_w, batch, ch, n_cols), out...  81.5 us
    unnamed x4, local copies, waits for them, and re-layouts  5.16 us

profile of v5, /device:TPU:97, one launch (start us, length us, event | category | flops | bytes accessed | tf_op | source)
XLA Modules:
  0.0 87.3 jit_solution(7781414253409352222)
XLA Ops:
  0.6 81.5 %convgru.1 = (bf16[4,1024,384]{2,1,0:T(8,128)(2,1)}, f32[16,64,384]{2,1,0:T(8,128)}) custom-call(bf16[4,1024,384]{2,1,0:T(8,128)(2,1)} %bitcast.9, f32[16,64,384]{2,1,0:T(8,128)} %bitcast.12, bf16[3456,1152]{1,0:T(8,128)(2,1)} %bitcast.7, bf16[3456,768]{1,0:T(8,128)(2,1)} %bitcast.8, bf16[3456,384]{1,0:T(8,128)(2,1)} %bitcast.11, f32[1152]{0:T(1024)} %bias.1), custom_call_target="tpu_custom_call" | custom-call | tf_op jit(solution)/shard_map/convgru/pallas_call | solution.py:375
  82.2 0.0 copy-start
  82.2 4.0 %copy.10 = bf16[4,16,8,8,384]{4,3,2,1,0:T(8,128)(2,1)} copy(bf16[4,16,8,8,384]{4,3,2,1,0:T(8,128)(2,1)} %bitcast.10) | data formatting | bytes 6291456
  86.2 0.0 copy-done
  86.2 1.1 %copy.11 = f32[16,8,8,384]{3,2,1,0:T(8,128)} copy(f32[16,8,8,384]{3,2,1,0:T(8,128)S(1)} %bitcast.13) | data formatting | bytes 3145728
Async XLA Ops:
  82.2 4.0 %copy-start = (f32[16,64,384]{2,1,0:T(8,128)S(1)}, f32[16,64,384]{2,1,0:T(8,128)}, u32[]{:S(2)}) copy-start(f32[16,64,384]{2,1,0:T(8,128)} %get-tuple-element.5) | copy-start | bytes 4718596

commit v6 on v5

--- a/solution.py
+++ b/solution.py
@@ -19,7 +19,7 @@
     half_w = tile_w // 2
 
     def kernel(frames, h0, wx, wz, wn, bias, h_seq, h_last,
-               xs, hs, ob, pm, xb, hb, rb, hf, zf, gv, wxv, wzv, wnv, send_sem, recv_sem, load_sem, out_sem):
+               xs, hs, pm, xb, hb, rb, hf, zf, gv, wxv, wzv, wnv, send_sem, recv_sem, load_sem):
         row = lax.axis_index('rows')
         col = lax.axis_index('cols')
         other = 1 - row
@@ -254,13 +254,10 @@
                         hf[r, c, :, g * L:(g + 1) * L] = v
                         hb[0, 1 + r, 1 + c, :, g * L:(g + 1) * L] = v.astype(BF)
 
-        def round_state():
+        def round_state(t):
             for b in range(batch):
                 for g in range(ch // L):
-                    ob[b * tile_h * tile_w:(b + 1) * tile_h * tile_w, g * L:(g + 1) * L] = hs[g, b, 0:tile_h * tile_w].astype(BF)
-
-        def store_step(t):
-            return pltpu.make_async_copy(ob, h_seq.at[t], out_sem.at[0])
+                    h_seq[t, b * tile_h * tile_w:(b + 1) * tile_h * tile_w, g * L:(g + 1) * L] = hs[g, b, 0:tile_h * tile_w].astype(BF)
 
         h_slot, r_slot = steps, steps + 2
 
@@ -302,11 +299,9 @@
             finish(1, both_b, inner_far, end_b(par))
             finish(2, both_c, inner_far, end_c(par))
             put(0, [(xb, t, wxv, 0)])
-            round_state()
+            round_state(jnp.maximum(t - 1, 0))
             wait_cols(xb, t, t)
             wait_cols(hb, par, h_slot + par)
-            store = store_step(jnp.maximum(t - 1, 0))
-            store.start()
             both_a = [(xb, t, wxv, 0), (hb, par, wzv, 0)]
             finish(1, both_b, edge_far, end_b(par))
             finish(2, both_c, edge_far, end_c(par))
@@ -338,7 +333,6 @@
             finish(3, both_d, inner_far, end_d(nxt))
             finish(4, both_e, inner_far, end_e(nxt), n=L)
             wait_cols(rb, par, r_slot + par)
-            store.wait()
             finish(3, both_d, edge_far, end_d(nxt))
             finish(4, both_e, edge_far, end_e(nxt), n=L)
 
@@ -347,16 +341,9 @@
                 send(hb, nxt, h_slot + nxt)
                 wait_rows(xb, t + 1, t + 1)
 
-        store_last = [pltpu.make_async_copy(hs.at[g, :, pl.ds(0, tile_h * tile_w)], h_last.at[:, :, pl.ds(g * L, L)],
-                                            load_sem.at[s0 + 6 + g]) for g in range(ch // L)]
-        for cp in store_last:
-            cp.start()
-        round_state()
-        store = store_step(steps - 1)
-        store.start()
-        for cp in store_last:
-            cp.wait()
-        store.wait()
+        round_state(steps - 1)
+        for g in range(ch // L):
+            h_last[:, :, g * L:(g + 1) * L] = hs[g, :, 0:tile_h * tile_w]
 
     return kernel
 
@@ -374,21 +361,20 @@
         any_spec = pl.BlockSpec(memory_space=pl.ANY)
         h_seq, h_last = pl.pallas_call(
             make_kernel(steps, tile_h, tile_w, batch, ch, n_cols),
-            out_shape=(jax.ShapeDtypeStruct((steps, tile_h * tile_w * batch, ch), BF),
-                       jax.ShapeDtypeStruct((batch, tile_h * tile_w, ch), F32)),
+            out_shape=(vmem((steps, tile_h * tile_w * batch, ch), BF), vmem((batch, tile_h * tile_w, ch), F32)),
             in_specs=[any_spec] * 5 + [pl.BlockSpec(memory_space=pltpu.VMEM)],
-            out_specs=(any_spec, any_spec),
+            out_specs=(pl.BlockSpec(memory_space=pltpu.VMEM),) * 2,
             scratch_shapes=[
                 vmem((steps, tile_h * tile_w * batch, ch), BF), vmem((ch // L, batch, tile_h * tile_w + 8, L), F32),
-                vmem((tile_h * tile_w * batch, ch), BF), vmem((2 * tile_w * batch, 2 * tile_w * batch), BF),
+                vmem((2 * tile_w * batch, 2 * tile_w * batch), BF),
                 vmem((steps,) + pad, BF), vmem((2,) + pad, BF), vmem((2,) + pad, BF),
                 vmem(tile, F32), vmem(tile, F32),
                 vmem((5,) + tile[:3] + (256,), F32),
                 vmem((9 * ch, 3 * ch), BF), vmem((9 * ch, 2 * ch), BF), vmem((9 * ch, ch), BF),
                 pltpu.SemaphoreType.DMA((steps + 4, 5)), pltpu.SemaphoreType.DMA((steps + 4, 5)),
-                pltpu.SemaphoreType.DMA((steps + 10,)), pltpu.SemaphoreType.DMA((1,)),
+                pltpu.SemaphoreType.DMA((steps + 10,)),
             ],
-            compiler_params=pltpu.CompilerParams(collective_id=0, has_side_effects=True, vmem_limit_bytes=60 * 1024 * 1024),
+            compiler_params=pltpu.CompilerParams(collective_id=0, has_side_effects=True, vmem_limit_bytes=52 * 1024 * 1024),
             name='convgru',
         )(
             frames.reshape(steps, -1, ch), h_init.reshape(batch, -1, ch),

time: 87.5 us -> 83.9 us (0.959)
  local copies, waits for them, and re-layouts: 5.16 us -> 2.81 us
  Pallas kernels: 81.5 us -> 80.3 us
    unnamed x4 -> x2, local copies, waits for them, and re-layouts: 5.16 us -> 2.81 us
    pallas_call x1, Pallas kernels: 81.5 us -> 80.3 us  [local_fn(): pl.pallas_call(make_kernel(steps, tile_h, tile_w, batch, ch, n_cols), out...]
where the time goes in v6:
time: 83.9 us; the launch traced here: 83.7 us
  Pallas kernels  80.3 us (96%)
  local copies, waits for them, and re-layouts  2.81 us (3%)
    pallas_call x1, Pallas kernels, local_fn(): pl.pallas_call(make_kernel(steps, tile_h, tile_w, batch, ch, n_cols), out...  80.3 us
    unnamed x2, local copies, waits for them, and re-layouts  2.81 us

profile of v6, /device:TPU:97, one launch (start us, length us, event | category | flops | bytes accessed | tf_op | source)
XLA Modules:
  0.0 83.7 jit_solution(3136560896051454956)
XLA Ops:
  0.6 80.3 %convgru.1 = (bf16[4,1024,384]{2,1,0:T(8,128)(2,1)S(1)}, f32[16,64,384]{2,1,0:T(8,128)S(1)}) custom-call(bf16[4,1024,384]{2,1,0:T(8,128)(2,1)} %bitcast.11, f32[16,64,384]{2,1,0:T(8,128)} %bitcast.13, bf16[3456,1152]{1,0:T(8,128)(2,1)} %bitcast.9, bf16[3456,768]{1,0:T(8,128)(2,1)} %bitcast.10, bf16[3456,384]{1,0:T(8,128)(2,1)} %bitcast.12, f32[1152]{0:T(1024)} %bias.1), custom_call_target="tpu_custom_call" | custom-call | tf_op jit(solution)/shard_map/convgru/pallas_call | solution.py:362
  80.9 1.7 %copy.10 = bf16[4,16,8,8,384]{4,3,2,1,0:T(8,128)(2,1)} copy(bf16[4,16,8,8,384]{4,3,2,1,0:T(8,128)(2,1)S(1)} %bitcast.7) | data formatting | bytes 6291456
  82.6 1.1 %copy.11 = f32[16,8,8,384]{3,2,1,0:T(8,128)} copy(f32[16,8,8,384]{3,2,1,0:T(8,128)S(1)} %bitcast.8) | data formatting | bytes 3145728

commit v7 on v6

--- a/solution.py
+++ b/solution.py
@@ -15,11 +15,34 @@
     return 0.5 * jnp.tanh(0.5 * v) + 0.5
 
 
+def round_state(hs, seq, t):
+    groups, batch, _, _ = hs.shape
+    cells = seq.shape[1] // batch
+    for b in range(batch):
+        for g in range(groups):
+            seq[t, b * cells:(b + 1) * cells, g * L:(g + 1) * L] = hs[g, b, 0:cells].astype(BF)
+
+
+def write_kernel(seq, hs, h_seq, h_last, final_seq, sem):
+    steps = h_seq.shape[0]
+    groups, _, _, _ = hs.shape
+    cells = h_last.shape[1]
+    cps = [pltpu.make_async_copy(seq.at[t], h_seq.at[t], sem.at[t]) for t in range(steps - 1)]
+    cps += [pltpu.make_async_copy(hs.at[g, :, pl.ds(0, cells)], h_last.at[:, :, pl.ds(g * L, L)], sem.at[steps + g]) for g in range(groups)]
+    for cp in cps:
+        cp.start()
+    round_state(hs, final_seq, 0)
+    cps.append(pltpu.make_async_copy(final_seq.at[0], h_seq.at[steps - 1], sem.at[steps - 1]))
+    cps[-1].start()
+    for cp in cps:
+        cp.wait()
+
+
 def make_kernel(steps, tile_h, tile_w, batch, ch, n_cols):
     half_w = tile_w // 2
 
-    def kernel(frames, h0, wx, wz, wn, bias, h_seq, h_last,
-               xs, hs, pm, xb, hb, rb, hf, zf, gv, wxv, wzv, wnv, send_sem, recv_sem, load_sem):
+    def kernel(frames, h0, wx, wz, wn, bias, seq, hs,
+               xs, pm, xb, hb, rb, hf, zf, gv, wxv, wzv, wnv, send_sem, recv_sem, load_sem):
         row = lax.axis_index('rows')
         col = lax.axis_index('cols')
         other = 1 - row
@@ -62,14 +85,10 @@
         load_frame(0).start()
         for cp in load_h:
             cp.start()
-        load_xbc.start()
         for t in range(1, steps):
             load_frame(t).start()
-        load_xa.start()
-        load_z.start()
-        load_xd.start()
-        load_xe.start()
-        load_n.start()
+        for cp in (load_xbc, load_xa, load_z, load_xd, load_xe, load_n):
+            cp.start()
 
         def zero_border(buf, i):
             buf[i, (tile_h + 1) * row] = jnp.zeros((tile_w + 3, batch, ch), BF)
@@ -254,11 +273,6 @@
                         hf[r, c, :, g * L:(g + 1) * L] = v
                         hb[0, 1 + r, 1 + c, :, g * L:(g + 1) * L] = v.astype(BF)
 
-        def round_state(t):
-            for b in range(batch):
-                for g in range(ch // L):
-                    h_seq[t, b * tile_h * tile_w:(b + 1) * tile_h * tile_w, g * L:(g + 1) * L] = hs[g, b, 0:tile_h * tile_w].astype(BF)
-
         h_slot, r_slot = steps, steps + 2
 
         make_permutation()
@@ -299,7 +313,7 @@
             finish(1, both_b, inner_far, end_b(par))
             finish(2, both_c, inner_far, end_c(par))
             put(0, [(xb, t, wxv, 0)])
-            round_state(jnp.maximum(t - 1, 0))
+            round_state(hs, seq, jnp.maximum(t - 1, 0))
             wait_cols(xb, t, t)
             wait_cols(hb, par, h_slot + par)
             both_a = [(xb, t, wxv, 0), (hb, par, wzv, 0)]
@@ -341,10 +355,6 @@
                 send(hb, nxt, h_slot + nxt)
                 wait_rows(xb, t + 1, t + 1)
 
-        round_state(steps - 1)
-        for g in range(ch // L):
-            h_last[:, :, g * L:(g + 1) * L] = hs[g, :, 0:tile_h * tile_w]
-
     return kernel
 
 
@@ -358,14 +368,15 @@
         pad = (tile_h + 2, tile_w + 3, batch, ch)
         tile = (tile_h, tile_w, batch, ch)
         vmem = pltpu.VMEM
+        cells = tile_h * tile_w
         any_spec = pl.BlockSpec(memory_space=pl.ANY)
-        h_seq, h_last = pl.pallas_call(
+        seq, staged = pl.pallas_call(
             make_kernel(steps, tile_h, tile_w, batch, ch, n_cols),
-            out_shape=(vmem((steps, tile_h * tile_w * batch, ch), BF), vmem((batch, tile_h * tile_w, ch), F32)),
+            out_shape=(vmem((steps - 1, cells * batch, ch), BF), vmem((ch // L, batch, cells + 8, L), F32)),
             in_specs=[any_spec] * 5 + [pl.BlockSpec(memory_space=pltpu.VMEM)],
             out_specs=(pl.BlockSpec(memory_space=pltpu.VMEM),) * 2,
             scratch_shapes=[
-                vmem((steps, tile_h * tile_w * batch, ch), BF), vmem((ch // L, batch, tile_h * tile_w + 8, L), F32),
+                vmem((steps, cells * batch, ch), BF),
                 vmem((2 * tile_w * batch, 2 * tile_w * batch), BF),
                 vmem((steps,) + pad, BF), vmem((2,) + pad, BF), vmem((2,) + pad, BF),
                 vmem(tile, F32), vmem(tile, F32),
@@ -380,6 +391,15 @@
             frames.reshape(steps, -1, ch), h_init.reshape(batch, -1, ch),
             w_x.reshape(9 * ch, -1), w_hzr.reshape(9 * ch, -1), w_hn.reshape(9 * ch, -1), gate_bias,
         )
+        h_seq, h_last = pl.pallas_call(
+            write_kernel,
+            out_shape=(jax.ShapeDtypeStruct((steps, cells * batch, ch), BF), jax.ShapeDtypeStruct((batch, cells, ch), F32)),
+            in_specs=[pl.BlockSpec(memory_space=pltpu.VMEM)] * 2,
+            out_specs=(any_spec, any_spec),
+            scratch_shapes=[vmem((1, cells * batch, ch), BF), pltpu.SemaphoreType.DMA((steps + ch // L,))],
+            compiler_params=pltpu.CompilerParams(vmem_limit_bytes=8 * 1024 * 1024),
+            name='write_out',
+        )(seq, staged)
         return h_seq.reshape(frames.shape), h_last.reshape(h_init.shape)
 
     return jax.shard_map(local_fn, mesh=mesh, in_specs=(frame_spec, state_spec, P(), P(), P(), P()),

time: 83.9 us -> 83.1 us (level)
  local copies, waits for them, and re-layouts: 2.81 us -> 0 us
  Pallas kernels: 80.3 us -> 82.3 us
    unnamed x2 -> x0, local copies, waits for them, and re-layouts: 2.81 us -> none
    pallas_call x0 -> x1, Pallas kernels: none -> 2.24 us  [local_fn(): pl.pallas_call(write_kernel, out_shape=(jax.ShapeDtypeStruct((steps, cell...]
where the time goes in v7:
time: 83.1 us; the launch traced here: 82.9 us
  Pallas kernels  82.3 us (99%)
    pallas_call x1, Pallas kernels, local_fn(): pl.pallas_call(make_kernel(steps, tile_h, tile_w, batch, ch, n_cols), out...  80.1 us
    pallas_call x1, Pallas kernels, local_fn(): pl.pallas_call(write_kernel, out_shape=(jax.ShapeDtypeStruct((steps, cell...  2.24 us

profile of v7, /device:TPU:97, one launch (start us, length us, event | category | flops | bytes accessed | tf_op | source)
XLA Modules:
  0.0 82.9 jit_solution(2668515297608029063)
XLA Ops:
  0.6 80.1 %convgru.1 = (bf16[3,1024,384]{2,1,0:T(8,128)(2,1)S(1)}, f32[3,16,72,128]{3,2,1,0:T(8,128)S(1)}) custom-call(bf16[4,1024,384]{2,1,0:T(8,128)(2,1)} %bitcast.9, f32[16,64,384]{2,1,0:T(8,128)} %bitcast.11, bf16[3456,1152]{1,0:T(8,128)(2,1)} %bitcast.7, bf16[3456,768]{1,0:T(8,128)(2,1)} %bitcast.8, bf16[3456,384]{1,0:T(8,128)(2,1)} %bitcast.10, f32[1152]{0:T(1024)} %bias.1), custom_call_target="tpu_custom_call" | custom-call | tf_op jit(solution)/shard_map/convgru/pallas_call | solution.py:373
  80.7 2.2 %write_out.1 = (bf16[4,1024,384]{2,1,0:T(8,128)(2,1)}, f32[16,64,384]{2,1,0:T(8,128)}) custom-call(bf16[3,1024,384]{2,1,0:T(8,128)(2,1)S(1)} %get-tuple-element.6.seq, f32[3,16,72,128]{3,2,1,0:T(8,128)S(1)} %get-tuple-element.7.hs), custom_call_target="tpu_custom_call" | custom-call | tf_op jit(solution)/shard_map/write_out/pallas_call | solution.py:394

commit v8 on v7

--- a/solution.py
+++ b/solution.py
@@ -315,11 +315,13 @@
             put(0, [(xb, t, wxv, 0)])
             round_state(hs, seq, jnp.maximum(t - 1, 0))
             wait_cols(xb, t, t)
+            add(1, [(xb, t, wxv, 256)], which=edge_far)
+            add(2, [(xb, t, wxv, 512)], which=edge_far)
             wait_cols(hb, par, h_slot + par)
             both_a = [(xb, t, wxv, 0), (hb, par, wzv, 0)]
-            finish(1, both_b, edge_far, end_b(par))
-            finish(2, both_c, edge_far, end_c(par))
-            add(0, both_a, which=edge_far)
+            finish(1, [(hb, par, wzv, 256)], edge_far, end_b(par))
+            finish(2, [(hb, par, wzv, 512)], edge_far, end_c(par))
+            add(0, [(hb, par, wzv, 0)], which=edge_far)
             send(rb, par, r_slot + par)
 
             @pl.when(t < steps - 1)
@@ -334,8 +336,7 @@
 
             add(0, [(hb, par, wzv, 0)])
             finish(0, both_a, inner_far, end_a)
-            for (_, c0, c1) in edge_far:
-                end_a(gv[slot_at(0, c0, c1, 256)], c0, c1)
+            finish(0, [(xb, t, wxv, 0)], edge_far, end_a)
             put(3, [(xb, t, wxv, 768)])
             wait_rows(rb, par, r_slot + par)
 
@@ -346,9 +347,11 @@
             put(4, both_e, n=L)
             finish(3, both_d, inner_far, end_d(nxt))
             finish(4, both_e, inner_far, end_e(nxt), n=L)
+            add(3, [(xb, t, wxv, 768)], which=edge_far)
+            add(4, [(xb, t, wxv, 1024)], n=L, which=edge_far)
             wait_cols(rb, par, r_slot + par)
-            finish(3, both_d, edge_far, end_d(nxt))
-            finish(4, both_e, edge_far, end_e(nxt), n=L)
+            finish(3, [(rb, par, wnv, 0)], edge_far, end_d(nxt))
+            finish(4, [(rb, par, wnv, 256)], edge_far, end_e(nxt), n=L)
 
             @pl.when(t < steps - 1)
             def _():

time: 83.1 us -> 84.2 us (1.013)
  Pallas kernels: 82.3 us -> 83.5 us
    pallas_call x1, Pallas kernels: 80.1 us -> 81.2 us  [local_fn(): pl.pallas_call(make_kernel(steps, tile_h, tile_w, batch, ch, n_cols), out...]
where the time goes in v8:
time: 84.2 us; the launch traced here: 84.1 us
  Pallas kernels  83.5 us (99%)
    pallas_call x1, Pallas kernels, local_fn(): pl.pallas_call(make_kernel(steps, tile_h, tile_w, batch, ch, n_cols), out...  81.2 us
    pallas_call x1, Pallas kernels, local_fn(): pl.pallas_call(write_kernel, out_shape=(jax.ShapeDtypeStruct((steps, cell...  2.24 us

profile of v8, /device:TPU:97, one launch (start us, length us, event | category | flops | bytes accessed | tf_op | source)
XLA Modules:
  0.0 84.1 jit_solution(4611823348754992516)
XLA Ops:
  0.6 81.2 %convgru.1 = (bf16[3,1024,384]{2,1,0:T(8,128)(2,1)S(1)}, f32[3,16,72,128]{3,2,1,0:T(8,128)S(1)}) custom-call(bf16[4,1024,384]{2,1,0:T(8,128)(2,1)} %bitcast.9, f32[16,64,384]{2,1,0:T(8,128)} %bitcast.11, bf16[3456,1152]{1,0:T(8,128)(2,1)} %bitcast.7, bf16[3456,768]{1,0:T(8,128)(2,1)} %bitcast.8, bf16[3456,384]{1,0:T(8,128)(2,1)} %bitcast.10, f32[1152]{0:T(1024)} %bias.1), custom_call_target="tpu_custom_call" | custom-call | tf_op jit(solution)/shard_map/convgru/pallas_call | solution.py:376
  81.9 2.2 %write_out.1 = (bf16[4,1024,384]{2,1,0:T(8,128)(2,1)}, f32[16,64,384]{2,1,0:T(8,128)}) custom-call(bf16[3,1024,384]{2,1,0:T(8,128)(2,1)S(1)} %get-tuple-element.6.seq, f32[3,16,72,128]{3,2,1,0:T(8,128)S(1)} %get-tuple-element.7.hs), custom_call_target="tpu_custom_call" | custom-call | tf_op jit(solution)/shard_map/write_out/pallas_call | solution.py:397
